TPU v7x, 256 devices: a whole 4x4x8 slice. The times are simulated.
256 devices in a mesh: expert: 128 (over y, z, x), tensor: 2 (over core).
Axes of the slice: x: 4, y: 4, z: 8, core: 2. Of those that a mesh axis runs over, the one named last changes fastest.
Arguments:
- states: bfloat16 [16384, 1536], P('expert'), may hold values from -60 to 60
- norm_gain: float32 [1536], replicated, may hold values from 0.25 to 1.75
- router: bfloat16 [1536, 64], replicated, may hold values from -0.15625 to 0.15625
- w_gate: bfloat16 [128, 1536, 2048], P('expert', None, 'tensor'), may hold values from -0.15625 to 0.15625
- w_up: bfloat16 [128, 1536, 2048], P('expert', None, 'tensor'), may hold values from -0.15625 to 0.15625
- w_down: bfloat16 [128, 2048, 1536], P('expert', 'tensor'), may hold values from -0.09375 to 0.09375
- expert_ids: int32 [16384, 2], P('expert'), may hold values from 0 to 63, as said below
- slot_pos: int32 [16384, 2], P('expert'), may hold values from 0 to 6, as said below
- keep_mask: int32 [16384, 2], P('expert'), may hold values from 0 to 1, as said below
Outputs:
- next_states: bfloat16 [16384, 1536], P('expert')
Inputs may be any that keep to these rules, and one draw needn't show every extreme that they name: `expert_ids`: each row names two different experts; in every block of 128 rows one expert is named by more than 6 rows. `slot_pos`: for each choice, the number of earlier choices of the same expert within the same block of 128 rows, counted row by row with a row's first choice before its second, or 6 where that number is 6 or more. `keep_mask`: 1 exactly where slot_pos is under 6; in every block of 128 rows some expert has all 6 slots filled.
All inputs are finite; a program needn't handle non-finite values.
Results may differ from a plain program's by a relative error of at most 0.0038.
Values may be sent and summed in bfloat16 or wider, within the bound.
No kernel may reach another device: no remote copies, remote signals or barrier semaphores. Data moves between devices by JAX's collectives and lax.ppermute only.
A program may use at most 64 MiB of HBM per device.

v0:
```python
import jax
import jax.numpy as jnp
from jax import lax
from jax.sharding import PartitionSpec as P


def in_order(parts, dim):
    parts = jnp.moveaxis(parts, 0, dim)
    shape = parts.shape
    return parts.reshape(*shape[:dim], shape[dim] * shape[dim + 1], *shape[dim + 2 :])


def from_everyone(x, axis):
    devices = lax.axis_size(axis)
    return lax.all_to_all(jnp.broadcast_to(x[None], (devices, *x.shape)), axis, 0, 0, tiled=True)


def gather_directly(x, axis, dim):
    return in_order(from_everyone(x, axis), dim)


def cut_along(x, dim, devices):
    before, after = (x.shape[:dim], x.shape[dim + 1 :])
    return jnp.moveaxis(x.reshape(*before, devices, -1, *after), dim, 0)


def sum_at_owner(x, axis, dim):
    devices = lax.axis_size(axis)
    parts = lax.all_to_all(cut_along(x, dim, devices), axis, 0, 0, tiled=True)
    return jnp.sum(parts.astype(jnp.float32), axis=0)


def per_device(states, norm_gain, router, w_gate, w_up, w_down, expert_ids, slot_pos, keep_mask):
    tok_rows, feat_width = states.shape
    groups = lax.axis_size("expert")
    all_experts = router.shape[1]
    holders = groups // all_experts
    capacity = max(2, 5 * tok_rows // (2 * all_experts) + 1)
    tensor_count = lax.axis_size("tensor")
    share_width = feat_width // tensor_count
    tensor_rank = lax.axis_index("tensor")
    values = states.astype(jnp.float32)
    normed = (
        values * lax.rsqrt(jnp.mean(values * values, axis=-1, keepdims=True) + 1e-06) * norm_gain
    ).astype(jnp.bfloat16)
    logits = jnp.dot(normed, router, preferred_element_type=jnp.float32)
    columns = lax.broadcasted_iota(jnp.int32, (tok_rows, all_experts), 1)
    chosen = jnp.stack(
        [
            jnp.sum(jnp.where(columns == expert_ids[:, pick][:, None], logits, 0.0), axis=1)
            for pick in range(expert_ids.shape[1])
        ],
        axis=1,
    )
    gate_score = jax.nn.sigmoid(chosen)
    weight = gate_score / jnp.sum(gate_score, axis=1, keepdims=True)
    is_kept = keep_mask > 0
    slot_index = jnp.where(is_kept, expert_ids * capacity + slot_pos, -1)
    targets = lax.broadcasted_iota(jnp.int32, (all_experts * capacity, tok_rows), 0)
    dispatch_table = jnp.any(targets[:, :, None] == slot_index[None, :, :], axis=-1).astype(
        jnp.bfloat16
    )
    source = lax.dynamic_slice_in_dim(normed, tensor_rank * share_width, share_width, 1)
    outgoing = jnp.dot(dispatch_table, source, preferred_element_type=jnp.float32).astype(
        jnp.bfloat16
    )
    outgoing = jnp.repeat(outgoing.reshape(all_experts, capacity, share_width), holders, axis=0)
    arrived = lax.all_to_all(outgoing, "expert", split_axis=0, concat_axis=0, tiled=True)
    arrived = gather_directly(arrived, "tensor", 2)
    flat_rows = arrived.reshape(groups * capacity, feat_width)
    gate_act = jnp.dot(flat_rows, w_gate[0], preferred_element_type=jnp.float32)
    up_act = jnp.dot(flat_rows, w_up[0], preferred_element_type=jnp.float32)
    hidden = (jax.nn.silu(gate_act) * up_act).astype(jnp.bfloat16)
    partial_out = jnp.dot(hidden, w_down[0], preferred_element_type=jnp.float32)
    partial_out = partial_out.reshape(groups, capacity, feat_width)
    summed = sum_at_owner(partial_out.astype(jnp.bfloat16), "tensor", 2)
    returned = lax.all_to_all(
        summed.astype(jnp.bfloat16), "expert", split_axis=0, concat_axis=0, tiled=True
    ).astype(summed.dtype)
    residual = lax.dynamic_slice_in_dim(values, tensor_rank * share_width, share_width, 1)
    out_width = returned.shape[2]
    expert_out = jnp.sum(
        returned.reshape(all_experts, holders, capacity, out_width), axis=1
    ).astype(jnp.bfloat16)
    flat_out = expert_out.reshape(all_experts * capacity, out_width)
    picked = jnp.take(flat_out, jnp.maximum(slot_index, 0), axis=0).astype(jnp.float32)
    factor = jnp.where(is_kept, weight, 0.0)
    combined = jnp.sum(factor[:, :, None] * picked, axis=1)
    next_states = (residual + combined).astype(jnp.bfloat16)
    next_states = gather_directly(next_states, "tensor", 1)
    return next_states


def solution(mesh):
    placed = (
        P("expert", None),
        P(),
        P(),
        P("expert", None, "tensor"),
        P("expert", None, "tensor"),
        P("expert", "tensor", None),
        P("expert", None),
        P("expert", None),
        P("expert", None),
    )
    return jax.shard_map(
        per_device, mesh=mesh, in_specs=placed, out_specs=P("expert", None), check_vma=False
    )
```

profile of v0, /device:TPU:1, one launch (start us, length us, event | category | flops | bytes accessed | tf_op | source)
XLA Modules:
  0.0 176.4 jit_solution(1059581206012020190)
XLA Ops:
  0.0 0.0 copy-start
  0.0 1.5 broadcast_compare_fusion
  1.5 1.2 multiply_reduce_fusion.1
  2.7 1.2 multiply_convert_fusion.1
  3.9 0.0 copy-start.2
  3.9 0.7 copy-done.2
  4.6 1.1 convolution_convert_fusion.1
  5.7 2.1 %reshape.42 = bf16[64,6,768]{2,1,0:T(8,128)(2,1)} reshape(bf16[384,768]{1,0:T(8,128)(2,1)} %convolution_convert_fusion.1) | data formatting | bytes 1179648 | tf_op jit(solution)/shard_map/reshape | solution.py:67
  7.8 1.2 broadcast_in_dim.50
  9.0 54.9 %all_to_all.25 = bf16[128,6,768]{2,1,0:T(8,128)(2,1)S(1)} all-to-all(bf16[128,6,768]{2,1,0:T(8,128)(2,1)S(1)} %bitcast.43), channel_id=1, replica_groups=mesh['expert'=128,'tensor'=2] {'expert'}, dimensions={0} | all-to-all | bytes 2359296 | tf_op jit(solution)/shard_map/all_to_all | solution.py:68
  64.0 0.2 copy.67
  64.2 0.2 broadcast_in_dim.51
  64.4 8.8 %all_to_all.26 = bf16[2,128,6,768]{3,1,2,0:T(8,128)(2,1)S(1)} all-to-all(bf16[2,128,6,768]{3,1,2,0:T(8,128)(2,1)S(1)} %broadcast_in_dim.51), channel_id=1, replica_groups=mesh['expert'=128,'tensor'=2] {'tensor'}, dimensions={0} | all-to-all | bytes 4718592 | tf_op jit(solution)/shard_map/all_to_all | solution.py:15
  73.2 2.4 %copy.68 = bf16[128,6,2,768]{3,2,1,0:T(2,128)(2,1)S(1)} copy(bf16[128,6,2,768]{3,0,1,2:T(8,128)(2,1)S(1)} %bitcast.40) | data formatting | bytes 4718592 | tf_op jit(solution)/shard_map/transpose | solution.py:8
  75.7 0.0 copy-start.5
  75.7 0.4 copy.81
  76.1 1.4 copy-done.5
  77.5 0.0 copy-start.6
  77.6 2.6 %fusion.3 = f32[768,1024]{1,0:T(8,128)S(1)} fusion(bf16[768,1536]{1,0:T(8,128)(2,1)S(1)} %bitcast.44, bf16[1,1536,1024]{2,1,0:T(8,128)(2,1)S(1)} %copy-done.5), kind=kOutput, calls=%fused_computation.5 | convolution fusion | flops 2415919104 | bytes 8650752 | tf_op jit(solution)/shard_map/dot_general | solution.py:71
  80.1 0.0 copy-done.6
  80.2 4.1 %multiply_convert_fusion = bf16[768,1024]{1,0:T(8,128)(2,1)} fusion(f32[768,1024]{1,0:T(8,128)S(1)} %fusion.3, bf16[768,1536]{1,0:T(8,128)(2,1)S(1)} %bitcast.45, bf16[1,1536,1024]{2,1,0:T(8,128)(2,1)S(1)} %copy-done.6), kind=kOutput, calls=%fused_computation.7 | convolution fusion | flops 2420637696 | bytes 10223616 | tf_op jit(solution)/shard_map/dot_general | solution.py:72
  84.2 3.7 %dot_general.21 = bf16[128,6,1024]{2,1,0:T(8,128)(2,1)} reshape(bf16[768,1024]{1,0:T(8,128)(2,1)} %multiply_convert_fusion) | data formatting | bytes 3145728 | tf_op jit(solution)/shard_map/dot_general | solution.py:74
  87.9 0.0 copy-done
  88.0 7.1 %convolution_convert_fusion = bf16[128,6,1536]{2,0,1:T(8,128)(2,1)S(1)} fusion(bf16[1,1024,1536]{2,1,0:T(8,128)(2,1)S(1)} %copy-done, bf16[128,6,1024]{2,1,0:T(8,128)(2,1)} %dot_general.21), kind=kOutput, calls=%fused_computation.1 | convolution fusion | flops 2417098752 | bytes 7077888 | tf_op jit(solution)/shard_map/dot_general | solution.py:74
  95.0 0.2 copy.85
  95.3 6.5 %all_to_all.27 = bf16[2,128,6,768]{3,1,2,0:T(8,128)(2,1)} all-to-all(bf16[2,128,6,768]{3,1,2,0:T(8,128)(2,1)S(1)} %bitcast.42), channel_id=1, replica_groups=mesh['expert'=128,'tensor'=2] {'tensor'}, dimensions={0} | all-to-all | bytes 4718592 | tf_op jit(solution)/shard_map/all_to_all | solution.py:29
  101.8 3.4 %reduce_sum.70 = bf16[128,6,768]{2,0,1:T(8,128)(2,1)} reduce(bf16[2,128,6,768]{3,1,2,0:T(8,128)(2,1)} %all_to_all.27, bf16[]{:T(256)} %constant.44.clone.1), dimensions={0}, to_apply=%region_5.6 | reduce | flops 589824 | bytes 3538946 | tf_op jit(solution)/shard_map/reduce_sum | solution.py:30
  105.2 3.1 %copy.72 = bf16[128,6,768]{2,1,0:T(8,128)(2,1)} copy(bf16[128,6,768]{2,0,1:T(8,128)(2,1)} %reduce_sum.70) | data formatting | bytes 2359296 | tf_op jit(solution)/shard_map/reduce_sum | solution.py:30
  108.3 7.6 %all-to-all-start.3 = ((bf16[128,6,768]{2,1,0:T(8,128)(2,1)}), bf16[128,6,768]{2,1,0:T(8,128)(2,1)}, u32[]{:S(2)}, u32[]{:S(2)}) async-start(bf16[128,6,768]{2,1,0:T(8,128)(2,1)} %copy.72), calls=%async_computation.3 | async-start | bytes 3145728 | tf_op jit(solution)/shard_map/all_to_all | solution.py:77
  115.9 0.0 copy-done.1
  115.9 1.0 convert_element_type.32
  116.9 0.1 copy.75
  117.0 0.1 reshape.50
  117.2 0.0 copy-done.4
  117.2 1.3 select_reduce_fusion.1
  118.5 0.0 copy-done.3
  118.5 0.8 copy.65
  119.3 0.8 copy.66
  120.1 34.0 %all-to-all-done.3 = bf16[128,6,768]{2,1,0:T(8,128)(2,1)} async-done(((bf16[128,6,768]{2,1,0:T(8,128)(2,1)}), bf16[128,6,768]{2,1,0:T(8,128)(2,1)}, u32[]{:S(2)}, u32[]{:S(2)}) %all-to-all-start.3) | async-done | bytes 1179680 | tf_op jit(solution)/shard_map/all_to_all | solution.py:77
  154.2 2.9 %bitcast_reduce_fusion = bf16[64,6,768]{2,1,0:T(8,128)(2,1)} fusion(bf16[128,6,768]{2,1,0:T(8,128)(2,1)} %all-to-all-done.3), kind=kLoop, calls=%fused_computation.9 | loop fusion | flops 294912 | bytes 1769472 | tf_op jit(solution)/shard_map/reduce_sum | solution.py:82
  157.0 2.1 %convert_element_type.38 = bf16[384,768]{1,0:T(8,128)(2,1)} reshape(bf16[64,6,768]{2,1,0:T(8,128)(2,1)} %bitcast_reduce_fusion) | data formatting | bytes 1179648 | tf_op jit(solution)/shard_map/convert_element_type | solution.py:84
  159.1 3.3 %gather_fusion = bf16[256,768]{1,0:T(8,128)(2,1)} fusion(bf16[384,768]{1,0:T(8,128)(2,1)} %convert_element_type.38, s32[1024]{0:T(1024)S(1)} %pad_clamp_fusion), kind=kCustom, calls=%fused_computation | custom fusion | bytes 787456 | tf_op jit(solution)/shard_map/jit(_take)/gather | solution.py:86
  162.4 1.1 reshape.49
  163.5 2.1 %multiply_reduce_fusion = f32[128,768]{1,0:T(8,128)S(1)} fusion(bf16[128,2,768]{2,1,0:T(2,128)(2,1)S(1)} %reshape.49, pred[128,2]{1,0:T(8,128)(4,1)S(1)} %copy.66, f32[128,2]{1,0:T(8,128)} %copy.65), kind=kLoop, calls=%fused_computation.12 | loop fusion | flops 688128 | bytes 787712 | tf_op jit(solution)/shard_map/reduce_sum | solution.py:88
  165.6 1.1 add_convert_fusion
  166.8 6.9 %all_to_all.28 = bf16[2,128,768]{2,1,0:T(8,128)(2,1)S(1)} all-to-all(bf16[2,128,768]{2,1,0:T(8,128)(2,1)S(1)} %broadcast_in_dim.54), channel_id=1, replica_groups=mesh['expert'=128,'tensor'=2] {'tensor'}, dimensions={0} | all-to-all | bytes 786432 | tf_op jit(solution)/shard_map/all_to_all | solution.py:15
  173.6 0.9 copy.76
  174.5 1.9 %copy.77 = bf16[128,1536]{1,0:T(8,128)(2,1)} copy(bf16[128,1536]{0,1:T(8,128)(2,1)} %bitcast.47) | data formatting | bytes 786432 | tf_op jit(solution)/shard_map/reshape | solution.py:10
  (11 shorter events, 0.1 us)
Async XLA Ops:
  0.0 87.9 %copy-start = (bf16[1,1024,1536]{2,1,0:T(8,128)(2,1)S(1)}, bf16[1,1024,1536]{2,1,0:T(8,128)(2,1)}, u32[]{:S(2)}) copy-start(bf16[1,1024,1536]{2,1,0:T(8,128)(2,1)} %param.14) | copy-start | bytes 9437188
  3.9 0.7 copy-start.2
  75.7 1.9 %copy-start.5 = (bf16[1,1536,1024]{2,1,0:T(8,128)(2,1)S(1)}, bf16[1,1536,1024]{2,1,0:T(8,128)(2,1)}, u32[]{:S(2)}) copy-start(bf16[1,1536,1024]{2,1,0:T(8,128)(2,1)} %param.12) | copy-start | bytes 9437188
  77.5 2.6 %copy-start.6 = (bf16[1,1536,1024]{2,1,0:T(8,128)(2,1)S(1)}, bf16[1,1536,1024]{2,1,0:T(8,128)(2,1)}, u32[]{:S(2)}) copy-start(bf16[1,1536,1024]{2,1,0:T(8,128)(2,1)} %param.13) | copy-start | bytes 9437188
  105.2 10.8 %copy-start.1 = (bf16[128,1536]{1,0:T(8,128)(2,1)S(1)}, bf16[128,1536]{1,0:T(8,128)(2,1)}, u32[]{:S(2)}) copy-start(bf16[128,1536]{1,0:T(8,128)(2,1)} %param.9) | copy-start | bytes 1179652
  108.3 8.9 %copy-start.4 = (s32[128,2]{0,1:T(2,128)S(1)}, s32[128,2]{0,1:T(2,128)}, u32[]{:S(2)}) copy-start(s32[128,2]{0,1:T(2,128)} %param.15) | copy-start | bytes 3076
  108.3 10.2 %copy-start.3 = (s32[128,2]{0,1:T(2,128)S(1)}, s32[128,2]{0,1:T(2,128)}, u32[]{:S(2)}) copy-start(s32[128,2]{0,1:T(2,128)} %param.17) | copy-start | bytes 3076
  108.3 45.9 %all-to-all-start.3 = ((bf16[128,6,768]{2,1,0:T(8,128)(2,1)}), bf16[128,6,768]{2,1,0:T(8,128)(2,1)}, u32[]{:S(2)}, u32[]{:S(2)}) async-start(bf16[128,6,768]{2,1,0:T(8,128)(2,1)} %copy.72), calls=%async_computation.3 | async-start | bytes 3145728 | tf_op jit(solution)/shard_map/all_to_all | solution.py:77
where the time goes:
time: 177 us; the launch traced here: 176 us
  blocking collectives  77.1 us (44%)
  waiting for transfers between devices  34 us (19%)
  local copies, waits for them, and re-layouts  27 us (15%)
  matrix products  16.2 us (9%)
  other arithmetic  14.3 us (8%)
  starting transfers between devices  7.61 us (4%)
    all_to_all x1, blocking collectives, per_device(): lax.all_to_all(outgoing, 'expert', split_axis=0, concat_axis=0, tiled=True)  54.9 us
    all_to_all x1, waiting for transfers between devices, per_device(): lax.all_to_all(summed.astype(jnp.bfloat16), 'expert', split_axis=0, conca...  34 us
    all_to_all x2, blocking collectives, from_everyone(): lax.all_to_all(jnp.broadcast_to(x[None], (devices, *x.shape)), axis, 0, 0...  15.7 us
    all_to_all x1, starting transfers between devices, per_device(): lax.all_to_all(summed.astype(jnp.bfloat16), 'expert', split_axis=0, conca...  7.61 us
    dot_general x1, matrix products, per_device(): partial_out = jnp.dot(hidden, w_down[0], preferred_element_type=jnp.float32)  7.07 us
    all_to_all x1, blocking collectives, sum_at_owner(): parts = lax.all_to_all(cut_along(x, dim, devices), axis, 0, 0, tiled=True)  6.5 us
    gather x2, local copies, waits for them, and re-layouts, per_device(): jnp.take(flat_out, jnp.maximum(slot_index, 0), axis=0).astype(jnp.float32)  4.42 us
    dot_general x1, matrix products, per_device(): up_act = jnp.dot(flat_rows, w_up[0], preferred_element_type=jnp.float32)  4.08 us
  transfers between devices with their start and end apart: 1, of which 1 were waited for; matrix products, arithmetic and copies ran while one was open for 2% of the time, Pallas kernels for 0%

commit v1 on v0

v1 whole, which is shorter than its diff:
```python
import jax
import jax.numpy as jnp
from jax import lax
from jax.sharding import PartitionSpec as P

CHUNKS = ((0, 1, 2),)
SWAP = ((0, 1), (1, 0))


def swap(x):
    return lax.ppermute(x, "tensor", SWAP)


def dot(a, b):
    return jnp.dot(a, b, preferred_element_type=jnp.float32)


def per_device(states, norm_gain, router, w_gate, w_up, w_down, expert_ids, slot_pos, keep_mask):
    tok_rows, width = states.shape
    groups = lax.axis_size("expert")
    all_experts = router.shape[1]
    holders = groups // all_experts
    capacity = max(2, 5 * tok_rows // (2 * all_experts) + 1)
    own_slots = capacity // 2
    first_slot = lax.axis_index("tensor") * own_slots

    gates = (w_gate[0], swap(w_gate)[0])
    ups = (w_up[0], swap(w_up)[0])
    downs = (w_down[0], swap(w_down)[0])

    values = states.astype(jnp.float32)
    normed = (
        values * lax.rsqrt(jnp.mean(values * values, axis=-1, keepdims=True) + 1e-06) * norm_gain
    ).astype(jnp.bfloat16)
    is_kept = keep_mask > 0
    slot_index = jnp.where(is_kept, expert_ids * capacity + slot_pos, -1)
    key = lax.broadcasted_iota(jnp.int32, (groups, tok_rows), 0) // holders * capacity + first_slot

    def send(chunk):
        rows = []
        for j in chunk:
            hit = (key + j == slot_index[:, 0][None, :]) | (key + j == slot_index[:, 1][None, :])
            rows.append(dot(hit.astype(jnp.bfloat16), normed).astype(jnp.bfloat16))
        rows = jnp.concatenate(rows, axis=1)
        return lax.all_to_all(rows, "expert", 0, 0, tiled=True)

    def ffn(arrived, chunk):
        rows = jnp.concatenate(
            [arrived[:, n * width : (n + 1) * width] for n in range(len(chunk))], axis=0
        )
        total = 0.0
        for g, u, d in zip(gates, ups, downs):
            hidden = (jax.nn.silu(dot(rows, g)) * dot(rows, u)).astype(jnp.bfloat16)
            total = total + dot(hidden, d)
        total = total.astype(jnp.bfloat16)
        back = jnp.concatenate(
            [total[n * groups : (n + 1) * groups] for n in range(len(chunk))], axis=1
        )
        return lax.all_to_all(back, "expert", 0, 0, tiled=True)

    arrived = [send(c) for c in CHUNKS]

    logits = dot(normed, router)
    columns = lax.broadcasted_iota(jnp.int32, (tok_rows, all_experts), 1)
    chosen = jnp.stack(
        [
            jnp.sum(jnp.where(columns == expert_ids[:, pick][:, None], logits, 0.0), axis=1)
            for pick in range(2)
        ],
        axis=1,
    )
    gate_score = jax.nn.sigmoid(chosen)
    weight = gate_score / jnp.sum(gate_score, axis=1, keepdims=True)
    key_t = lax.broadcasted_iota(jnp.int32, (tok_rows, groups), 1) // holders * capacity + first_slot

    returned = [ffn(a, c) for a, c in zip(arrived, CHUNKS)]

    partial = 0.0
    for back, chunk in zip(returned, CHUNKS):
        for n, j in enumerate(chunk):
            share = sum(
                jnp.where(key_t + j == slot_index[:, k][:, None], weight[:, k][:, None], 0.0)
                for k in range(2)
            )
            high = lax.reduce_precision(share, 8, 7)
            low = (share - high).astype(jnp.bfloat16)
            rows = back[:, n * width : (n + 1) * width]
            partial = partial + dot(high.astype(jnp.bfloat16), rows) + dot(low, rows)
    mine = partial.astype(jnp.bfloat16)
    other = swap(mine)
    mine = lax.reduce_precision(partial, 8, 7)
    return (values + (mine + other.astype(jnp.float32))).astype(jnp.bfloat16)


def solution(mesh):
    placed = (
        P("expert", None),
        P(),
        P(),
        P("expert", None, "tensor"),
        P("expert", None, "tensor"),
        P("expert", "tensor", None),
        P("expert", None),
        P("expert", None),
        P("expert", None),
    )
    return jax.shard_map(
        per_device, mesh=mesh, in_specs=placed, out_specs=P("expert", None), check_vma=False
    )
```

time: 177 us -> 142 us (0.80)
  blocking collectives: 77.1 us -> 0 us
  starting transfers between devices: 7.61 us -> 32.6 us
  waiting for transfers between devices: 34 us -> 58.3 us
  matrix products: 16.2 us -> 25 us
  local copies, waits for them, and re-layouts: 27 us -> 18.6 us
  other arithmetic: 14.3 us -> 6.09 us
    all_to_all x4 -> x0, blocking collectives: 77.1 us -> none  [the longest x1 54.9 us: per_device(): lax.all_to_all(outgoing, 'expert', split_axis=0, concat_axis=0, tiled=True)]
    all_to_all x1 -> x2, waiting for transfers between devices: 34 us -> 57 us  [the longest x1 28.9 us: ffn(): return lax.all_to_all(back, 'expert', 0, 0, tiled=True)]
    all_to_all x1 -> x2, starting transfers between devices: 7.61 us -> 26.8 us  [the longest x1 16.8 us: send(): return lax.all_to_all(rows, 'expert', 0, 0, tiled=True)]
    unnamed x15 -> x16, local copies, waits for them, and re-layouts: 2.64 us -> 17.9 us
    dot_general x5 -> x14, matrix products: 16.2 us -> 25 us  [dot(): return jnp.dot(a, b, preferred_element_type=jnp.float32)]
    reduce_sum x3 -> x0, other arithmetic: 8.39 us -> none  [the longest x1 3.41 us: sum_at_owner(): return jnp.sum(parts.astype(jnp.float32), axis=0)]
    ppermute x0 -> x4, starting transfers between devices: none -> 5.85 us  [swap(): return lax.ppermute(x, 'tensor', SWAP)]
    gather x2 -> x0, local copies, waits for them, and re-layouts: 4.42 us -> none  [per_device(): jnp.take(flat_out, jnp.maximum(slot_index, 0), axis=0).astype(jnp.float32)]
  transfers between devices with their start and end apart: 1 -> 6, of which waited for: 1 -> 3; matrix products, arithmetic and copies ran while one was open for 2% -> 14% of each run, Pallas kernels for 0% -> 0%
where the time goes in v1:
time: 142 us; the launch traced here: 141 us
  waiting for transfers between devices  58.3 us (41%)
  starting transfers between devices  32.6 us (23%)
  matrix products  25 us (18%)
  local copies, waits for them, and re-layouts  18.6 us (13%)
  other arithmetic  6.09 us (4%)
    all_to_all x1, waiting for transfers between devices, ffn(): return lax.all_to_all(back, 'expert', 0, 0, tiled=True)  28.9 us
    all_to_all x1, waiting for transfers between devices, send(): return lax.all_to_all(rows, 'expert', 0, 0, tiled=True)  28.1 us
    dot_general x14, matrix products, dot(): return jnp.dot(a, b, preferred_element_type=jnp.float32)  25 us
    unnamed x16, local copies, waits for them, and re-layouts  17.9 us
    all_to_all x1, starting transfers between devices, send(): return lax.all_to_all(rows, 'expert', 0, 0, tiled=True)  16.8 us
    all_to_all x1, starting transfers between devices, ffn(): return lax.all_to_all(back, 'expert', 0, 0, tiled=True)  9.98 us
    ppermute x4, starting transfers between devices, swap(): return lax.ppermute(x, 'tensor', SWAP)  5.85 us
  transfers between devices with their start and end apart: 6, of which 3 were waited for; matrix products, arithmetic and copies ran while one was open for 14% of the time, Pallas kernels for 0%

profile of v1, /device:TPU:1, one launch (start us, length us, event | category | flops | bytes accessed | tf_op | source)
XLA Modules:
  0.0 140.9 jit_solution(6898224258919770892)
XLA Ops:
  0.0 0.0 copy-start
  0.0 0.8 compare_select_fusion
  0.8 1.2 fusion.22
  2.0 1.4 convolution_convert_fusion.1
  3.4 1.4 convolution_convert_fusion.2
  4.7 0.0 copy-done.1
  4.7 0.0 copy-done.4
  4.7 0.4 convolution_convert_fusion
  5.1 0.1 maximum_bitcast_fusion
  5.2 0.5 broadcast.131
  5.7 1.5 %reduce = bf16[128,4608]{1,0:T(8,128)(2,1)S(1)} reduce(bf16[128,1,4608]{2,0,1:T(8,128)(2,1)S(1)} %maximum_bitcast_fusion, bf16[]{:T(256)} %broadcast.131), dimensions={1}, to_apply=%copy.12.reduce_sub_computation | reduce | bytes 2359298 | tf_op jit(solution)/shard_map/all_to_all | solution.py:45
  7.2 1.2 reshape.16
  8.4 16.8 %all-to-all-start = ((bf16[128,2,2304]{2,1,0:T(2,128)(2,1)}), bf16[128,2,2304]{2,1,0:T(2,128)(2,1)}, u32[]{:S(2)}, u32[]{:S(2)}) async-start(bf16[128,2,2304]{2,1,0:T(2,128)(2,1)} %reshape.16), calls=%async_computation | async-start | bytes 2359296 | tf_op jit(solution)/shard_map/all_to_all | solution.py:45
  25.2 1.0 collective-permute-start.1
  26.2 0.1 collective-permute-start
  26.4 0.4 collective-permute-start.2
  26.8 28.1 %all-to-all-done = bf16[128,2,2304]{2,1,0:T(2,128)(2,1)} async-done(((bf16[128,2,2304]{2,1,0:T(2,128)(2,1)}), bf16[128,2,2304]{2,1,0:T(2,128)(2,1)}, u32[]{:S(2)}, u32[]{:S(2)}) %all-to-all-start) | async-done | bytes 1179680 | tf_op jit(solution)/shard_map/all_to_all | solution.py:45
  54.8 6.8 %reshape.17 = bf16[128,1,4608]{2,1,0:T(2,128)(2,1)S(1)} reshape(bf16[128,2,2304]{2,1,0:T(2,128)(2,1)} %all-to-all-done) | data formatting | bytes 2359296
  61.6 0.0 copy-start.3
  61.6 0.2 copy.19
  61.8 0.1 fusion.161
  61.9 1.6 %copy-done.3 = bf16[1,1536,1024]{2,1,0:T(8,128)(2,1)S(1)} copy-done((bf16[1,1536,1024]{2,1,0:T(8,128)(2,1)S(1)}, bf16[1,1536,1024]{2,1,0:T(8,128)(2,1)}, u32[]{:S(2)}) %copy-start.3) | copy-done | bytes 3145752
  63.5 1.4 fusion.10
  64.9 6.9 %fusion.6 = f32[384,1536]{1,0:T(8,128)} fusion(bf16[1,1024,1536]{2,1,0:T(8,128)(2,1)} %param.14, f32[384,1024]{1,0:T(8,128)S(1)} %fusion.10, bf16[1,1536,1024]{2,1,0:T(8,128)(2,1)} %param.13, bf16[128,1536]{1,0:T(8,128)(2,1)S(1)} %get-tuple-element.11, bf16[128,1536]{1,0:T(8,128)(2,1)S(1)} %get-tuple-element.12, bf16[128,1536]{1,0:T(8,128)(2,1)S(1)} %get-tuple-element.10), kind=kOutput, calls=%fused_computation.6 | convolution fusion | flops 2421817344 | bytes 11403264 | tf_op jit(solution)/shard_map/dot_general | solution.py:15
  71.8 0.0 collective-permute-done.1
  71.8 4.5 %fusion.2 = f32[384,1024]{1,0:T(8,128)} fusion(bf16[1,1536,1024]{2,1,0:T(8,128)(2,1)} %collective-permute-done.1, bf16[128,1536]{1,0:T(8,128)(2,1)S(1)} %get-tuple-element.11, bf16[128,1536]{1,0:T(8,128)(2,1)S(1)} %get-tuple-element.12, bf16[128,1536]{1,0:T(8,128)(2,1)S(1)} %get-tuple-element.10), kind=kOutput, calls=%fused_computation.2 | convolution fusion | flops 1211498496 | bytes 5898240 | tf_op jit(solution)/shard_map/dot_general | solution.py:15
  76.3 0.0 collective-permute-done
  76.4 0.0 collective-permute-done.2
  76.4 6.7 %fusion.15 = bf16[384,1536]{1,0:T(8,128)(2,1)S(1)} fusion(f32[384,1536]{1,0:T(8,128)} %fusion.6, bf16[1,1024,1536]{2,1,0:T(8,128)(2,1)} %collective-permute-done.2, f32[384,1024]{1,0:T(8,128)} %fusion.2, bf16[1,1536,1024]{2,1,0:T(8,128)(2,1)} %collective-permute-done, bf16[128,1536]{1,0:T(8,128)(2,1)S(1)} %get-tuple-element.11, ...), kind=kOutput, calls=%fused_computation.13 | convolution fusion | flops 2422996992 | bytes 12582912 | tf_op jit(solution)/shard_map/dot_general | solution.py:15
  83.1 0.1 fusion.160
  83.2 0.1 maximum_bitcast_fusion.1
  83.3 1.5 %reduce.1 = bf16[128,4608]{1,0:T(8,128)(2,1)S(1)} reduce(bf16[128,1,4608]{2,0,1:T(8,128)(2,1)S(1)} %maximum_bitcast_fusion.1, bf16[]{:T(256)} %broadcast.131), dimensions={1}, to_apply=%copy.13.reduce_sub_computation | reduce | bytes 2359298 | tf_op jit(solution)/shard_map/all_to_all | solution.py:59
  84.8 1.2 reshape.18
  86.0 10.0 %all-to-all-start.1 = ((bf16[128,2,2304]{2,1,0:T(2,128)(2,1)}), bf16[128,2,2304]{2,1,0:T(2,128)(2,1)}, u32[]{:S(2)}, u32[]{:S(2)}) async-start(bf16[128,2,2304]{2,1,0:T(2,128)(2,1)} %reshape.18), calls=%async_computation.1 | async-start | bytes 2359296 | tf_op jit(solution)/shard_map/all_to_all | solution.py:59
  96.0 0.0 copy-done.2
  96.0 0.3 select_reduce_fusion.1
  96.4 28.9 %all-to-all-done.1 = bf16[128,2,2304]{2,1,0:T(2,128)(2,1)} async-done(((bf16[128,2,2304]{2,1,0:T(2,128)(2,1)}), bf16[128,2,2304]{2,1,0:T(2,128)(2,1)}, u32[]{:S(2)}, u32[]{:S(2)}) %all-to-all-start.1) | async-done | bytes 1179680 | tf_op jit(solution)/shard_map/all_to_all | solution.py:59
  125.3 6.8 %reshape.19 = bf16[128,1,4608]{2,1,0:T(2,128)(2,1)S(1)} reshape(bf16[128,2,2304]{2,1,0:T(2,128)(2,1)} %all-to-all-done.1) | data formatting | bytes 2359296
  132.1 0.2 copy.18
  132.3 0.3 fusion.37
  132.6 0.3 convolution_add_fusion.4
  133.0 0.3 convolution_add_fusion.3
  133.3 0.3 convolution_add_fusion.2
  133.7 0.3 convolution_add_fusion.1
  134.0 0.3 fusion.162
  134.3 4.3 %collective-permute-start.3 = (bf16[128,1536]{1,0:T(8,128)(2,1)S(1)}, bf16[128,1536]{1,0:T(8,128)(2,1)S(1)}, u32[]{:S(2)}, u32[]{:S(2)}) collective-permute-start(bf16[128,1536]{1,0:T(8,128)(2,1)S(1)} %get-tuple-element.19), channel_id=1, source_target_pairs={{0,1},{1,0},{2,3},{3,2},{4,5},{5,4},{6,7},{7,6},{8,9},{9,8},{10,11... | collective-permute-start | bytes 1179656 | tf_op jit(solution)/shard_map/ppermute | solution.py:11
  138.6 1.3 collective-permute-done.3
  140.0 0.9 fusion.25
  (12 shorter events, 0.1 us)
Async XLA Ops:
  0.0 96.0 %copy-start = (bf16[1536,64]{0,1:T(8,128)(2,1)S(1)}, bf16[1536,64]{0,1:T(8,128)(2,1)}, u32[]{:S(2)}) copy-start(bf16[1536,64]{0,1:T(8,128)(2,1)} %param.11) | copy-start | bytes 589828
  0.0 4.7 %copy-start.1 = (bf16[128,1536]{1,0:T(8,128)(2,1)S(1)}, bf16[128,1536]{1,0:T(8,128)(2,1)}, u32[]{:S(2)}) copy-start(bf16[128,1536]{1,0:T(8,128)(2,1)} %param.9) | copy-start | bytes 1179652
  0.0 4.7 %copy-start.4 = (f32[1536]{0:T(1024)S(1)}, f32[1536]{0:T(1024)}, u32[]{:S(2)}) copy-start(f32[1536]{0:T(1024)} %param.10) | copy-start | bytes 18436
  8.4 46.4 %all-to-all-start = ((bf16[128,2,2304]{2,1,0:T(2,128)(2,1)}), bf16[128,2,2304]{2,1,0:T(2,128)(2,1)}, u32[]{:S(2)}, u32[]{:S(2)}) async-start(bf16[128,2,2304]{2,1,0:T(2,128)(2,1)} %reshape.16), calls=%async_computation | async-start | bytes 2359296 | tf_op jit(solution)/shard_map/all_to_all | solution.py:45
  25.2 46.6 %collective-permute-start.1 = (bf16[1,1536,1024]{2,1,0:T(8,128)(2,1)}, bf16[1,1536,1024]{2,1,0:T(8,128)(2,1)}, u32[]{:S(2)}, u32[]{:S(2)}) collective-permute-start(bf16[1,1536,1024]{2,1,0:T(8,128)(2,1)} %param.13), channel_id=1, source_target_pairs={{0,1},{1,0},{2,3},{3,2},{4,5},{5,4},{6,7},{7,6},{8,9},{9,8},{10,11... | collective-permute-start | bytes 9437192 | tf_op jit(solution)/shard_map/ppermute | solution.py:11
  26.2 50.1 %collective-permute-start = (bf16[1,1536,1024]{2,1,0:T(8,128)(2,1)}, bf16[1,1536,1024]{2,1,0:T(8,128)(2,1)}, u32[]{:S(2)}, u32[]{:S(2)}) collective-permute-start(bf16[1,1536,1024]{2,1,0:T(8,128)(2,1)} %param.12), channel_id=1, source_target_pairs={{0,1},{1,0},{2,3},{3,2},{4,5},{5,4},{6,7},{7,6},{8,9},{9,8},{10,11... | collective-permute-start | bytes 9437192 | tf_op jit(solution)/shard_map/ppermute | solution.py:11
  26.4 50.0 %collective-permute-start.2 = (bf16[1,1024,1536]{2,1,0:T(8,128)(2,1)}, bf16[1,1024,1536]{2,1,0:T(8,128)(2,1)}, u32[]{:S(2)}, u32[]{:S(2)}) collective-permute-start(bf16[1,1024,1536]{2,1,0:T(8,128)(2,1)} %param.14), channel_id=1, source_target_pairs={{0,1},{1,0},{2,3},{3,2},{4,5},{5,4},{6,7},{7,6},{8,9},{9,8},{10,11... | collective-permute-start | bytes 9437192 | tf_op jit(solution)/shard_map/ppermute | solution.py:11
  61.6 1.9 %copy-start.3 = (bf16[1,1536,1024]{2,1,0:T(8,128)(2,1)S(1)}, bf16[1,1536,1024]{2,1,0:T(8,128)(2,1)}, u32[]{:S(2)}) copy-start(bf16[1,1536,1024]{2,1,0:T(8,128)(2,1)} %param.12) | copy-start | bytes 9437188
  86.0 10.0 %copy-start.2 = (s32[128,2]{0,1:T(2,128)S(1)}, s32[128,2]{0,1:T(2,128)}, u32[]{:S(2)}) copy-start(s32[128,2]{0,1:T(2,128)} %param.15) | copy-start | bytes 3076
  86.0 39.3 %all-to-all-start.1 = ((bf16[128,2,2304]{2,1,0:T(2,128)(2,1)}), bf16[128,2,2304]{2,1,0:T(2,128)(2,1)}, u32[]{:S(2)}, u32[]{:S(2)}) async-start(bf16[128,2,2304]{2,1,0:T(2,128)(2,1)} %reshape.18), calls=%async_computation.1 | async-start | bytes 2359296 | tf_op jit(solution)/shard_map/all_to_all | solution.py:59
  134.3 5.6 %collective-permute-start.3 = (bf16[128,1536]{1,0:T(8,128)(2,1)S(1)}, bf16[128,1536]{1,0:T(8,128)(2,1)S(1)}, u32[]{:S(2)}, u32[]{:S(2)}) collective-permute-start(bf16[128,1536]{1,0:T(8,128)(2,1)S(1)} %get-tuple-element.19), channel_id=1, source_target_pairs={{0,1},{1,0},{2,3},{3,2},{4,5},{5,4},{6,7},{7,6},{8,9},{9,8},{10,11... | collective-permute-start | bytes 1179656 | tf_op jit(solution)/shard_map/ppermute | solution.py:11

commit v2 on v1

v2 whole, which is shorter than its diff:
```python
import functools

import jax
import jax.numpy as jnp
from jax import lax
from jax.experimental import pallas as pl
from jax.experimental.pallas import tpu as pltpu
from jax.sharding import PartitionSpec as P

SWAP = ((0, 1), (1, 0))
MIB = 1 << 20
BF16 = jnp.bfloat16
F32 = jnp.float32
VMEM = pl.BlockSpec(memory_space=pltpu.VMEM)
ANY = pl.BlockSpec(memory_space=pl.ANY)


def swap(x):
    return lax.ppermute(x, "tensor", SWAP)


def dot(a, b):
    return jnp.dot(a, b, preferred_element_type=F32)


def dispatch_kernel(first, holders, capacity, slots_own, states, gain, slots, normed_out, send):
    rows, width = states.shape
    groups = send.shape[0]
    values = states[...].astype(F32)
    mean = jnp.mean(values * values, axis=-1, keepdims=True)
    normed = (values * lax.rsqrt(mean + 1e-06) * gain[...]).astype(BF16)
    normed_out[...] = normed
    owner = lax.broadcasted_iota(jnp.int32, (groups, rows), 0) // holders * capacity
    half = width // 2
    for j in range(slots_own):
        key = owner + (first[0] + j)
        hit = (key == slots[0:1, :]) | (key == slots[1:2, :])
        moved = dot(jnp.where(hit, 1.0, 0.0).astype(BF16), normed).astype(BF16)
        send[:, :, j * half : (j + 1) * half] = moved.reshape(groups, 2, half)


def weights_kernel(first, holders, capacity, slots_own, normed, router, ids, slots, table):
    rows = normed.shape[0]
    experts = router.shape[0]
    groups = experts * holders
    logits = lax.dot_general(
        router[...], normed[...], (((1,), (1,)), ((), ())), preferred_element_type=F32
    )
    expert = lax.broadcasted_iota(jnp.int32, (experts, rows), 0)
    score = []
    for k in range(2):
        chosen = jnp.sum(jnp.where(expert == ids[k : k + 1, :], logits, 0.0), axis=0, keepdims=True)
        score.append(1.0 / (1.0 + jnp.exp(-chosen)))
    total = score[0] + score[1]
    owner = lax.broadcasted_iota(jnp.int32, (groups, rows), 0) // holders * capacity
    for j in range(slots_own):
        key = owner + (first[0] + j)
        share = jnp.where(key == slots[0:1, :], score[0] / total, 0.0)
        share = share + jnp.where(key == slots[1:2, :], score[1] / total, 0.0)
        share = share.T
        high = share.astype(BF16)
        low = (share - high.astype(F32)).astype(BF16)
        table[:, (2 * j) * groups : (2 * j + 1) * groups] = high
        table[:, (2 * j + 1) * groups : (2 * j + 2) * groups] = low


def expert_kernel(slots_own, arrived, *refs):
    hbm, (back, rows, hidden, out, gates, ups, downs, sems) = refs[:6], refs[6:]
    groups = arrived.shape[0]
    width = rows.shape[1]
    part = gates.shape[2]
    piece = part // 2
    half = width // 2
    copies = []

    def start(src, dst):
        copy = pltpu.make_async_copy(src, dst, sems.at[len(copies)])
        copy.start()
        copies.append(copy)
        return copy

    loads = []
    for s in range(2):
        for p in range(2):
            cols = slice(p * piece, (p + 1) * piece)
            g = start(hbm[3 * s].at[:, cols], gates.at[s, :, cols])
            u = start(hbm[3 * s + 1].at[:, cols], ups.at[s, :, cols])
            loads.append((g, u))
    down_loads = [start(hbm[3 * s + 2], downs.at[s]) for s in range(2)]
    for j in range(slots_own):
        rows[j * groups : (j + 1) * groups, :] = arrived[:, :, j * half : (j + 1) * half].reshape(
            groups, width
        )
    for s in range(2):
        for p in range(2):
            for copy in loads[2 * s + p]:
                copy.wait()
            for q in range(piece // 256):
                lo = p * piece + q * 256
                gate = dot(rows[...], gates[s, :, lo : lo + 256])
                up = dot(rows[...], ups[s, :, lo : lo + 256])
                hidden[:, s * part + lo : s * part + lo + 256] = (
                    gate / (1.0 + jnp.exp(-gate)) * up
                ).astype(BF16)
    for copy in down_loads:
        copy.wait()
    for n in range(width // 256):
        cols = slice(n * 256, (n + 1) * 256)
        total = dot(hidden[:, :part], downs[0, :, cols]) + dot(hidden[:, part:], downs[1, :, cols])
        out[:, cols] = total.astype(BF16)
    for j in range(slots_own):
        back[:, :, j * half : (j + 1) * half] = out[j * groups : (j + 1) * groups, :].reshape(
            groups, 2, half
        )


def combine_kernel(slots_own, table, returned, partial):
    groups = returned.shape[0]
    width = partial.shape[1]
    half = width // 2
    total = jnp.zeros(partial.shape, F32)
    for j in range(slots_own):
        rows = returned[:, :, j * half : (j + 1) * half].reshape(groups, width)
        high = table[:, (2 * j) * groups : (2 * j + 1) * groups]
        low = table[:, (2 * j + 1) * groups : (2 * j + 2) * groups]
        total = total + dot(high, rows) + dot(low, rows)
    partial[...] = total.astype(BF16)


def per_device(states, norm_gain, router, w_gate, w_up, w_down, expert_ids, slot_pos, keep_mask):
    rows, width = states.shape
    groups = lax.axis_size("expert")
    experts = router.shape[1]
    holders = groups // experts
    capacity = max(2, 5 * rows // (2 * experts) + 1)
    own = capacity // 2
    part = w_gate.shape[2]
    first = (lax.axis_index("tensor") * own).astype(jnp.int32).reshape(1)
    smem = pl.BlockSpec(memory_space=pltpu.SMEM)
    mine = (w_gate[0], w_up[0], w_down[0])
    theirs = tuple(swap(w)[0] for w in (w_gate, w_up, w_down))
    ids = expert_ids.T
    slots = jnp.where(keep_mask.T > 0, ids * capacity + slot_pos.T, -1)

    packet = jax.ShapeDtypeStruct((groups, 2, own * width // 2), BF16)
    normed, send = pl.pallas_call(
        lambda *refs: dispatch_kernel(refs[0], holders, capacity, own, *refs[1:]),
        out_shape=(jax.ShapeDtypeStruct(states.shape, BF16), packet),
        in_specs=[smem, VMEM, VMEM, VMEM],
        out_specs=(VMEM, VMEM),
        compiler_params=pltpu.CompilerParams(vmem_limit_bytes=24 * MIB),
        name="dispatch",
    )(first, states, norm_gain[None, :], slots)
    arrived = lax.all_to_all(send, "expert", 0, 0, tiled=True)
    table = pl.pallas_call(
        lambda *refs: weights_kernel(refs[0], holders, capacity, own, *refs[1:]),
        out_shape=jax.ShapeDtypeStruct((rows, own * 2 * groups), BF16),
        in_specs=[smem, VMEM, VMEM, VMEM, VMEM],
        out_specs=VMEM,
        compiler_params=pltpu.CompilerParams(vmem_limit_bytes=16 * MIB),
        cost_estimate=pl.CostEstimate(flops=2 * 10**9, bytes_accessed=10**6, transcendentals=0),
        name="weights",
    )(first, normed, router.T, ids, slots)
    back = pl.pallas_call(
        functools.partial(expert_kernel, own),
        out_shape=packet,
        in_specs=[VMEM] + [ANY] * 6,
        out_specs=VMEM,
        scratch_shapes=[
            pltpu.VMEM((own * groups, width), BF16),
            pltpu.VMEM((own * groups, 2 * part), BF16),
            pltpu.VMEM((own * groups, width), BF16),
            pltpu.VMEM((2, width, part), BF16),
            pltpu.VMEM((2, width, part), BF16),
            pltpu.VMEM((2, part, width), BF16),
            pltpu.SemaphoreType.DMA((10,)),
        ],
        compiler_params=pltpu.CompilerParams(vmem_limit_bytes=60 * MIB),
        cost_estimate=pl.CostEstimate(
            flops=12 * own * groups * width * part, bytes_accessed=20 * 10**6, transcendentals=0
        ),
        name="experts",
    )(arrived, *mine, *theirs)
    returned = lax.all_to_all(back, "expert", 0, 0, tiled=True)
    partial = pl.pallas_call(
        functools.partial(combine_kernel, own),
        out_shape=jax.ShapeDtypeStruct(states.shape, BF16),
        in_specs=[VMEM, VMEM],
        out_specs=VMEM,
        compiler_params=pltpu.CompilerParams(vmem_limit_bytes=16 * MIB),
        name="combine",
    )(table, returned)
    added = partial.astype(F32) + swap(partial).astype(F32)
    return (states.astype(F32) + added).astype(BF16)


def solution(mesh):
    placed = (
        P("expert", None),
        P(),
        P(),
        P("expert", None, "tensor"),
        P("expert", None, "tensor"),
        P("expert", "tensor", None),
        P("expert", None),
        P("expert", None),
        P("expert", None),
    )
    return jax.shard_map(
        per_device, mesh=mesh, in_specs=placed, out_specs=P("expert", None), check_vma=False
    )
```

time: 142 us -> 113 us (0.80)
  blocking collectives: 0 us -> 44.8 us
  waiting for transfers between devices: 58.3 us -> 30.9 us
  matrix products: 25 us -> 0 us
  starting transfers between devices: 32.6 us -> 16.5 us
  Pallas kernels: 0 us -> 15.9 us
  local copies, waits for them, and re-layouts: 18.6 us -> 3.32 us
  other arithmetic: 6.09 us -> 1.62 us
    all_to_all x0 -> x1, blocking collectives: none -> 44.8 us  [per_device(): arrived = lax.all_to_all(send, 'expert', 0, 0, tiled=True)]
    all_to_all x2 -> x1, waiting for transfers between devices: 57 us -> 29.5 us  [per_device(): returned = lax.all_to_all(back, 'expert', 0, 0, tiled=True)]
    dot_general x14 -> x0, matrix products: 25 us -> none  [dot(): return jnp.dot(a, b, preferred_element_type=jnp.float32)]
    all_to_all x2 -> x1, starting transfers between devices: 26.8 us -> 8.91 us  [per_device(): returned = lax.all_to_all(back, 'expert', 0, 0, tiled=True)]
    pallas_call x0 -> x4, Pallas kernels: none -> 15.9 us  [the longest x1 13.2 us: per_device(): pl.pallas_call(functools.partial(expert_kernel, own), out_shape=packet, i...]
    unnamed x16 -> x10, local copies, waits for them, and re-layouts: 17.9 us -> 2.62 us
    all_to_all x4 -> x0, other arithmetic: 3.19 us -> none  [the longest x2 1.59 us: ffn(): return lax.all_to_all(back, 'expert', 0, 0, tiled=True)]
    ppermute x4, starting transfers between devices: 5.85 us -> 7.6 us  [swap(): return lax.ppermute(x, 'tensor', SWAP)]
  transfers between devices with their start and end apart: 6 -> 5, of which waited for: 3 -> 2; matrix products, arithmetic and copies ran while one was open for 14% -> 1% of each run, Pallas kernels for 0% -> 2%
where the time goes in v2:
time: 113 us
  blocking collectives  44.8 us (40%)
  waiting for transfers between devices  30.9 us (27%)
  starting transfers between devices  16.5 us (15%)
  Pallas kernels  15.9 us (14%)
  local copies, waits for them, and re-layouts  3.32 us (3%)
  other arithmetic  1.62 us (1%)
    all_to_all x1, blocking collectives, per_device(): arrived = lax.all_to_all(send, 'expert', 0, 0, tiled=True)  44.8 us
    all_to_all x1, waiting for transfers between devices, per_device(): returned = lax.all_to_all(back, 'expert', 0, 0, tiled=True)  29.5 us
    pallas_call x1, Pallas kernels, per_device(): pl.pallas_call(functools.partial(expert_kernel, own), out_shape=packet, i...  13.2 us
    all_to_all x1, starting transfers between devices, per_device(): returned = lax.all_to_all(back, 'expert', 0, 0, tiled=True)  8.91 us
    ppermute x4, starting transfers between devices, swap(): return lax.ppermute(x, 'tensor', SWAP)  7.6 us
    unnamed x10, local copies, waits for them, and re-layouts  2.62 us
  transfers between devices with their start and end apart: 5, of which 2 were waited for; matrix products, arithmetic and copies ran while one was open for 1% of the time, Pallas kernels for 2%

profile of v2, /device:TPU:1, one launch (start us, length us, event | category | flops | bytes accessed | tf_op | source)
XLA Modules:
  0.0 113.1 jit_solution(13808794793214142189)
XLA Ops:
  0.0 3.2 %collective-permute-start = (bf16[1,1536,1024]{2,1,0:T(8,128)(2,1)}, bf16[1,1536,1024]{2,1,0:T(8,128)(2,1)S(1)}, u32[]{:S(2)}, u32[]{:S(2)}) collective-permute-start(bf16[1,1536,1024]{2,1,0:T(8,128)(2,1)} %param.12), channel_id=1, source_target_pairs={{0,1},{1,0},{2,3},{3,2},{4,5},{5,4},{6,7},{7,6},{8,9},{9,8},{10,11... | collective-permute-start | bytes 9437192 | tf_op jit(solution)/shard_map/ppermute | solution.py:19
  3.2 0.0 collective-permute-start.1
  3.2 0.5 collective-permute-start.2
  3.7 0.7 broadcast_in_dim.7.refs_2_
  4.4 0.7 bitcast_select_fusion.refs_3_.refs_4_
  5.1 0.0 copy-start
  5.1 1.0 copy-done
  6.1 1.4 %dispatch.1 = (bf16[128,1536]{1,0:T(8,128)(2,1)S(1)}, bf16[128,2,2304]{2,1,0:T(2,128)(2,1)S(1)}) custom-call(s32[1]{0:T(128)} %bitcast.refs_0_, bf16[128,1536]{1,0:T(8,128)(2,1)S(1)} %copy-done, f32[1,1536]{1,0:T(1,128)S(1)} %broadcast_in_dim.7.refs_2_, s32[2,128]{1,0:T(2,128)S(1)} %bitcast_select_fusion.refs_3_.refs_4_), custom_call_target="tpu_custom_call" | custom-call | tf_op jit(solution)/shard_map/dispatch/pallas_call | solution.py:146
  7.5 44.8 %all_to_all.10.arrived = bf16[128,2,2304]{2,1,0:T(2,128)(2,1)} all-to-all(bf16[128,2,2304]{2,1,0:T(2,128)(2,1)S(1)} %get-tuple-element.8), channel_id=1, replica_groups=mesh['expert'=128,'tensor'=2] {'expert'}, dimensions={0} | all-to-all | bytes 2359296 | tf_op jit(solution)/shard_map/all_to_all | solution.py:154
  52.3 0.0 collective-permute-done
  52.3 0.0 copy-start.4
  52.3 0.0 collective-permute-done.1
  52.3 0.0 collective-permute-done.2
  52.3 1.6 %copy-done.4 = bf16[1,1536,1024]{2,1,0:T(8,128)(2,1)} copy-done((bf16[1,1536,1024]{2,1,0:T(8,128)(2,1)}, bf16[1,1536,1024]{2,1,0:T(8,128)(2,1)S(1)}, u32[]{:S(2)}) %copy-start.4) | copy-done | bytes 3145752
  53.9 0.0 copy-start.2
  53.9 0.0 copy-start.3
  53.9 13.2 %experts.1 = bf16[128,2,2304]{2,1,0:T(2,128)(2,1)} custom-call(bf16[128,2,2304]{2,1,0:T(2,128)(2,1)} %all_to_all.10.arrived, bf16[1536,1024]{1,0:T(8,128)(2,1)} %bitcast.18, bf16[1536,1024]{1,0:T(8,128)(2,1)} %bitcast.19, bf16[1024,1536]{1,0:T(8,128)(2,1)} %bitcast.20, bf16[1536,1024]{1,0:T(8,128)(2,1)} %bitcast.21, bf16[1536,1024]{1,0:T(8,128)(2,1)} %bitcast.9.refs_4_, ...), custom_call_target="tpu_custom_call" | custom-call | flops 7247757312 | bytes 20000000 | tf_op jit(solution)/shard_map/experts/pallas_call | solution.py:164
  67.1 8.9 %all-to-all-start.1 = ((bf16[128,2,2304]{2,1,0:T(2,128)(2,1)}), bf16[128,2,2304]{2,1,0:T(2,128)(2,1)S(1)}, u32[]{:S(2)}, u32[]{:S(2)}) async-start(bf16[128,2,2304]{2,1,0:T(2,128)(2,1)} %experts.1), calls=%async_computation.1 | async-start | bytes 2359296 | tf_op jit(solution)/shard_map/all_to_all | solution.py:184
  76.1 0.0 copy-done.2
  76.1 0.0 copy-done.3
  76.1 0.0 copy-start.1
  76.1 0.4 weights.1.table
  76.5 29.5 %all-to-all-done.1.returned = bf16[128,2,2304]{2,1,0:T(2,128)(2,1)S(1)} async-done(((bf16[128,2,2304]{2,1,0:T(2,128)(2,1)}), bf16[128,2,2304]{2,1,0:T(2,128)(2,1)S(1)}, u32[]{:S(2)}, u32[]{:S(2)}) %all-to-all-start.1) | async-done | bytes 1179680 | tf_op jit(solution)/shard_map/all_to_all | solution.py:184
  106.0 0.9 combine.1
  106.9 3.9 %collective-permute-start.3 = (bf16[128,1536]{1,0:T(8,128)(2,1)S(1)}, bf16[128,1536]{1,0:T(8,128)(2,1)S(1)}, u32[]{:S(2)}, u32[]{:S(2)}) collective-permute-start(bf16[128,1536]{1,0:T(8,128)(2,1)S(1)} %combine.1), channel_id=1, source_target_pairs={{0,1},{1,0},{2,3},{3,2},{4,5},{5,4},{6,7},{7,6},{8,9},{9,8},{10,11... | collective-permute-start | bytes 1179656 | tf_op jit(solution)/shard_map/ppermute | solution.py:19
  110.8 1.3 %collective-permute-done.3 = bf16[128,1536]{1,0:T(8,128)(2,1)S(1)} collective-permute-done((bf16[128,1536]{1,0:T(8,128)(2,1)S(1)}, bf16[128,1536]{1,0:T(8,128)(2,1)S(1)}, u32[]{:S(2)}, u32[]{:S(2)}) %collective-permute-start.3) | collective-permute-done | bytes 393248 | tf_op jit(solution)/shard_map/ppermute | solution.py:19
  112.1 0.0 copy-done.1
  112.1 0.9 add_convert_fusion
Async XLA Ops:
  0.0 52.3 %collective-permute-start = (bf16[1,1536,1024]{2,1,0:T(8,128)(2,1)}, bf16[1,1536,1024]{2,1,0:T(8,128)(2,1)S(1)}, u32[]{:S(2)}, u32[]{:S(2)}) collective-permute-start(bf16[1,1536,1024]{2,1,0:T(8,128)(2,1)} %param.12), channel_id=1, source_target_pairs={{0,1},{1,0},{2,3},{3,2},{4,5},{5,4},{6,7},{7,6},{8,9},{9,8},{10,11... | collective-permute-start | bytes 9437192 | tf_op jit(solution)/shard_map/ppermute | solution.py:19
  3.2 49.1 %collective-permute-start.1 = (bf16[1,1536,1024]{2,1,0:T(8,128)(2,1)}, bf16[1,1536,1024]{2,1,0:T(8,128)(2,1)}, u32[]{:S(2)}, u32[]{:S(2)}) collective-permute-start(bf16[1,1536,1024]{2,1,0:T(8,128)(2,1)} %param.13), channel_id=1, source_target_pairs={{0,1},{1,0},{2,3},{3,2},{4,5},{5,4},{6,7},{7,6},{8,9},{9,8},{10,11... | collective-permute-start | bytes 9437192 | tf_op jit(solution)/shard_map/ppermute | solution.py:19
  3.2 49.1 %collective-permute-start.2 = (bf16[1,1024,1536]{2,1,0:T(8,128)(2,1)}, bf16[1,1024,1536]{2,1,0:T(8,128)(2,1)}, u32[]{:S(2)}, u32[]{:S(2)}) collective-permute-start(bf16[1,1024,1536]{2,1,0:T(8,128)(2,1)} %param.14), channel_id=1, source_target_pairs={{0,1},{1,0},{2,3},{3,2},{4,5},{5,4},{6,7},{7,6},{8,9},{9,8},{10,11... | collective-permute-start | bytes 9437192 | tf_op jit(solution)/shard_map/ppermute | solution.py:19
  5.1 1.0 copy-start
  52.3 1.6 %copy-start.4 = (bf16[1,1536,1024]{2,1,0:T(8,128)(2,1)}, bf16[1,1536,1024]{2,1,0:T(8,128)(2,1)S(1)}, u32[]{:S(2)}) copy-start(bf16[1,1536,1024]{2,1,0:T(8,128)(2,1)S(1)} %collective-permute-done) | copy-start | bytes 9437188
  53.9 22.2 %copy-start.2 = (s32[128,2]{0,1:T(2,128)S(1)}, s32[128,2]{0,1:T(2,128)}, u32[]{:S(2)}) copy-start(s32[128,2]{0,1:T(2,128)} %param.15) | copy-start | bytes 3076
  53.9 22.2 %copy-start.3 = (bf16[1536,64]{0,1:T(8,128)(2,1)S(1)}, bf16[1536,64]{0,1:T(8,128)(2,1)}, u32[]{:S(2)}) copy-start(bf16[1536,64]{0,1:T(8,128)(2,1)} %param.11) | copy-start | bytes 589828
  67.1 38.9 %all-to-all-start.1 = ((bf16[128,2,2304]{2,1,0:T(2,128)(2,1)}), bf16[128,2,2304]{2,1,0:T(2,128)(2,1)S(1)}, u32[]{:S(2)}, u32[]{:S(2)}) async-start(bf16[128,2,2304]{2,1,0:T(2,128)(2,1)} %experts.1), calls=%async_computation.1 | async-start | bytes 2359296 | tf_op jit(solution)/shard_map/all_to_all | solution.py:184
  76.1 36.1 %copy-start.1 = (bf16[128,1536]{1,0:T(8,128)(2,1)S(1)}, bf16[128,1536]{1,0:T(8,128)(2,1)}, u32[]{:S(2)}) copy-start(bf16[128,1536]{1,0:T(8,128)(2,1)} %refs_1_.1) | copy-start | bytes 1179652
  106.9 5.2 %collective-permute-start.3 = (bf16[128,1536]{1,0:T(8,128)(2,1)S(1)}, bf16[128,1536]{1,0:T(8,128)(2,1)S(1)}, u32[]{:S(2)}, u32[]{:S(2)}) collective-permute-start(bf16[128,1536]{1,0:T(8,128)(2,1)S(1)} %combine.1), channel_id=1, source_target_pairs={{0,1},{1,0},{2,3},{3,2},{4,5},{5,4},{6,7},{7,6},{8,9},{9,8},{10,11... | collective-permute-start | bytes 1179656 | tf_op jit(solution)/shard_map/ppermute | solution.py:19

commit v3 on v2

v3 whole, which is shorter than its diff:
```python
import functools

import jax
import jax.numpy as jnp
from jax import lax
from jax.experimental import pallas as pl
from jax.experimental.pallas import tpu as pltpu
from jax.sharding import Mesh, PartitionSpec as P

SWAP = ((0, 1), (1, 0))
AXES = (4, 8, 4)
MIB = 1 << 20
BF16 = jnp.bfloat16
F32 = jnp.float32
VMEM = pl.BlockSpec(memory_space=pltpu.VMEM)
ANY = pl.BlockSpec(memory_space=pl.ANY)


def swap(x):
    return lax.ppermute(x, "tensor", SWAP)


def dot(a, b):
    return jnp.dot(a, b, preferred_element_type=F32)


def iota(shape, dim):
    return lax.broadcasted_iota(jnp.int32, shape, dim)


def slot_keys(own, tokens):
    ys, zs, xs = AXES
    pairs = xs // 2
    shape = (zs, own, ys * pairs, tokens)
    inner = iota(shape, 2)
    expert = (inner // pairs * zs + iota(shape, 0)) * pairs + inner % pairs
    key = expert * (2 * own) + iota(shape, 1) + lax.axis_index("tensor") * own
    return key.reshape(zs * own * ys * pairs, tokens)


def slot_numbers(own, ids, pos, keep):
    return jnp.where(keep[...] > 0, ids[...] * (2 * own) + pos[...], -1)


def dispatch_kernel(own, states, gain, ids, pos, keep, normed_out, send):
    tokens = states.shape[0]
    values = states[...].astype(F32)
    mean = jnp.mean(values * values, axis=-1, keepdims=True)
    normed = (values * lax.rsqrt(mean + 1e-06) * gain[...][None, :]).astype(BF16)
    normed_out[...] = normed
    slots = slot_numbers(own, ids, pos, keep)
    key = slot_keys(own, tokens)
    hit = (key == slots[0:1, :]) | (key == slots[1:2, :])
    send[...] = dot(jnp.where(hit, 1.0, 0.0).astype(BF16), normed).astype(BF16)


def regroup_kernel(own, arrived, send):
    ys, zs, xs = AXES
    experts = ys * xs // 2
    count = experts * own * zs
    shape = (experts, own, zs, count)
    source = (iota(shape, 2) * own + iota(shape, 1)) * experts + iota(shape, 0)
    pick = (source == iota(shape, 3)).reshape(count, count)
    rows = dot(jnp.where(pick, 1.0, 0.0).astype(BF16), arrived[...]).astype(BF16)
    size = own * zs
    for e in range(experts):
        for h in range(2):
            send[(2 * e + h) * size : (2 * e + h + 1) * size, :] = rows[e * size : (e + 1) * size, :]


def gather_kernel(own, partial, send):
    ys, zs, xs = AXES
    experts = ys * xs // 2
    count = experts * own * zs
    shape = (zs, own, experts, 2 * count)
    holder = (iota(shape, 2) * 2 * own + iota(shape, 1)) * zs + iota(shape, 0)
    column = iota(shape, 3)
    pick = ((column == holder) | (column == holder + own * zs)).reshape(count, 2 * count)
    send[...] = dot(jnp.where(pick, 1.0, 0.0).astype(BF16), partial[...]).astype(BF16)


def weights_kernel(own, normed, router, ids, pos, keep, table):
    tokens = normed.shape[0]
    experts = router.shape[0]
    logits = lax.dot_general(
        router[...], normed[...], (((1,), (1,)), ((), ())), preferred_element_type=F32
    )
    expert = iota((experts, tokens), 0)
    score = []
    for k in range(2):
        chosen = jnp.sum(jnp.where(expert == ids[k : k + 1, :], logits, 0.0), axis=0, keepdims=True)
        score.append(1.0 / (1.0 + jnp.exp(-chosen)))
    total = score[0] + score[1]
    slots = slot_numbers(own, ids, pos, keep)
    key = slot_keys(own, tokens)
    share = jnp.where(key == slots[0:1, :], score[0] / total, 0.0)
    share = share + jnp.where(key == slots[1:2, :], score[1] / total, 0.0)
    share = share.T
    high = share.astype(BF16)
    table[0] = high
    table[1] = (share - high.astype(F32)).astype(BF16)


def expert_kernel(rows, *refs):
    hbm, (back, hidden, gates, ups, downs, sems) = refs[:6], refs[6:]
    width = rows.shape[1]
    part = gates.shape[2]
    piece = part // 2
    copies = []

    def start(src, dst):
        copy = pltpu.make_async_copy(src, dst, sems.at[len(copies)])
        copy.start()
        copies.append(copy)
        return copy

    loads = []
    for s in range(2):
        for p in range(2):
            cols = slice(p * piece, (p + 1) * piece)
            g = start(hbm[3 * s].at[:, cols], gates.at[s, :, cols])
            u = start(hbm[3 * s + 1].at[:, cols], ups.at[s, :, cols])
            loads.append((g, u))
    down_loads = [
        start(hbm[3 * s + 2], downs.at[s * part : (s + 1) * part, :]) for s in range(2)
    ]
    for s in range(2):
        for p in range(2):
            for copy in loads[2 * s + p]:
                copy.wait()
            cols = slice(p * piece, (p + 1) * piece)
            gate = dot(rows[...], gates[s, :, cols])
            up = dot(rows[...], ups[s, :, cols])
            hidden[:, s * part + p * piece : s * part + (p + 1) * piece] = (
                gate / (1.0 + jnp.exp(-gate)) * up
            ).astype(BF16)
    for copy in down_loads:
        copy.wait()
    for n in range(width // 512):
        cols = slice(n * 512, (n + 1) * 512)
        back[:, cols] = dot(hidden[...], downs[:, cols]).astype(BF16)


def combine_kernel(table, returned, partial):
    partial[...] = (dot(table[0], returned[...]) + dot(table[1], returned[...])).astype(BF16)


def params(mib):
    return pltpu.CompilerParams(vmem_limit_bytes=mib * MIB)


def per_device(states, norm_gain, router, w_gate, w_up, w_down, expert_ids, slot_pos, keep_mask):
    tokens, width = states.shape
    ys, zs, xs = AXES
    experts = router.shape[1]
    own = max(2, 5 * tokens // (2 * experts) + 1) // 2
    part = w_gate.shape[2]
    chips = ys * xs
    once = own * experts
    rows = jax.ShapeDtypeStruct((once, width), BF16)
    twice = jax.ShapeDtypeStruct((2 * once, width), BF16)
    mine = (w_gate[0], w_up[0], w_down[0])
    theirs = tuple(swap(w)[0] for w in (w_gate, w_up, w_down))
    routing = (expert_ids.T, slot_pos.T, keep_mask.T)

    def along_z(x):
        x = x.reshape(zs, once // zs, width)
        return lax.all_to_all(x, "z", 0, 0, tiled=True).reshape(once, width)

    def in_plane(x):
        x = x.reshape(chips, 2 * once // chips, width)
        return lax.all_to_all(x, ("y", "x"), 0, 0, tiled=True).reshape(2 * once, width)

    normed, send = pl.pallas_call(
        functools.partial(dispatch_kernel, own),
        out_shape=(jax.ShapeDtypeStruct(states.shape, BF16), rows),
        in_specs=[VMEM] * 5,
        out_specs=(VMEM, VMEM),
        compiler_params=params(16),
        name="dispatch",
    )(states, norm_gain, *routing)
    column = along_z(send)
    table = pl.pallas_call(
        functools.partial(weights_kernel, own),
        out_shape=jax.ShapeDtypeStruct((2, tokens, once), BF16),
        in_specs=[VMEM] * 5,
        out_specs=VMEM,
        compiler_params=params(16),
        cost_estimate=pl.CostEstimate(flops=2 * 10**9, bytes_accessed=10**6, transcendentals=0),
        name="weights",
    )(normed, router.T, *routing)
    spread = pl.pallas_call(
        functools.partial(regroup_kernel, own),
        out_shape=twice,
        in_specs=[VMEM],
        out_specs=VMEM,
        compiler_params=params(16),
        name="regroup",
    )(column)
    arrived = in_plane(spread)
    back = pl.pallas_call(
        expert_kernel,
        out_shape=twice,
        in_specs=[VMEM] + [ANY] * 6,
        out_specs=VMEM,
        scratch_shapes=[
            pltpu.VMEM((2 * once, 2 * part), BF16),
            pltpu.VMEM((2, width, part), BF16),
            pltpu.VMEM((2, width, part), BF16),
            pltpu.VMEM((2 * part, width), BF16),
            pltpu.SemaphoreType.DMA((10,)),
        ],
        compiler_params=params(60),
        cost_estimate=pl.CostEstimate(
            flops=24 * once * width * part, bytes_accessed=20 * 10**6, transcendentals=0
        ),
        name="experts",
    )(arrived, *mine, *theirs)
    plane = in_plane(back)
    summed = pl.pallas_call(
        functools.partial(gather_kernel, own),
        out_shape=rows,
        in_specs=[VMEM],
        out_specs=VMEM,
        compiler_params=params(16),
        name="gather",
    )(plane)
    returned = along_z(summed)
    partial = pl.pallas_call(
        combine_kernel,
        out_shape=jax.ShapeDtypeStruct(states.shape, BF16),
        in_specs=[VMEM, VMEM],
        out_specs=VMEM,
        compiler_params=params(16),
        name="combine",
    )(table, returned)
    added = partial.astype(F32) + swap(partial).astype(F32)
    return (states.astype(F32) + added).astype(BF16)


def solution(mesh):
    grid = Mesh(mesh.devices.reshape(*AXES, 2), ("y", "z", "x", "tensor"))
    group = ("y", "z", "x")
    placed = (
        P(group, None),
        P(),
        P(),
        P(group, None, "tensor"),
        P(group, None, "tensor"),
        P(group, "tensor", None),
        P(group, None),
        P(group, None),
        P(group, None),
    )
    return jax.shard_map(
        per_device, mesh=grid, in_specs=placed, out_specs=P(group, None), check_vma=False
    )
```

time: 113 us -> 119 us (1.053)
  blocking collectives: 44.8 us -> 70.9 us
  waiting for transfers between devices: 30.9 us -> 17.6 us
  starting transfers between devices: 16.5 us -> 10.4 us
    all_to_all x1 -> x3, blocking collectives: 44.8 us -> 70.9 us  [the longest x2 45.2 us: in_plane(): lax.all_to_all(x, ('y', 'x'), 0, 0, tiled=True).reshape(2 * once, width)]
    all_to_all x1, waiting for transfers between devices: 29.5 us -> 16.2 us  [along_z(): return lax.all_to_all(x, 'z', 0, 0, tiled=True).reshape(once, width)]
    all_to_all x1, starting transfers between devices: 8.91 us -> 3.54 us  [along_z(): return lax.all_to_all(x, 'z', 0, 0, tiled=True).reshape(once, width)]
    unnamed x10 -> x20, local copies, waits for them, and re-layouts: 2.62 us -> 3.76 us
    pallas_call x4 -> x6, Pallas kernels: 15.9 us -> 15.3 us  [the longest x1 12.5 us: per_device(): pl.pallas_call(expert_kernel, out_shape=twice, in_specs=[VMEM] + [ANY] *...]
  transfers between devices with their start and end apart: 5 -> 5, of which waited for: 2 -> 2; matrix products, arithmetic and copies ran while one was open for 1% -> 0% of each run, Pallas kernels for 2% -> 1%
where the time goes in v3:
time: 119 us
  blocking collectives  70.9 us (60%)
  waiting for transfers between devices  17.6 us (15%)
  Pallas kernels  15.3 us (13%)
  starting transfers between devices  10.4 us (9%)
  local copies, waits for them, and re-layouts  3.76 us (3%)
    all_to_all x2, blocking collectives, in_plane(): lax.all_to_all(x, ('y', 'x'), 0, 0, tiled=True).reshape(2 * once, width)  45.2 us
    all_to_all x1, blocking collectives, along_z(): return lax.all_to_all(x, 'z', 0, 0, tiled=True).reshape(once, width)  25.7 us
    all_to_all x1, waiting for transfers between devices, along_z(): return lax.all_to_all(x, 'z', 0, 0, tiled=True).reshape(once, width)  16.2 us
    pallas_call x1, Pallas kernels, per_device(): pl.pallas_call(expert_kernel, out_shape=twice, in_specs=[VMEM] + [ANY] *...  12.5 us
    ppermute x4, starting transfers between devices, swap(): return lax.ppermute(x, 'tensor', SWAP)  6.89 us
    unnamed x20, local copies, waits for them, and re-layouts  3.76 us
    all_to_all x1, starting transfers between devices, along_z(): return lax.all_to_all(x, 'z', 0, 0, tiled=True).reshape(once, width)  3.54 us
  transfers between devices with their start and end apart: 5, of which 2 were waited for; matrix products, arithmetic and copies ran while one was open for 0% of the time, Pallas kernels for 1%

profile of v3, /device:TPU:1, one launch (start us, length us, event | category | flops | bytes accessed | tf_op | source)
XLA Modules:
  0.0 118.9 jit_solution(12333168849412036157)
XLA Ops:
  0.0 3.2 %collective-permute-start = (bf16[1,1536,1024]{2,1,0:T(8,128)(2,1)}, bf16[1,1536,1024]{2,1,0:T(8,128)(2,1)}, u32[]{:S(2)}, u32[]{:S(2)}) collective-permute-start(bf16[1,1536,1024]{2,1,0:T(8,128)(2,1)} %param.12), channel_id=1, source_target_pairs={{0,1},{1,0},{2,3},{3,2},{4,5},{5,4},{6,7},{7,6},{8,9},{9,8},{10,11... | collective-permute-start | bytes 9437192 | tf_op jit(solution)/shard_map/ppermute | solution.py:20
  3.2 0.0 collective-permute-start.1
  3.2 0.5 collective-permute-start.2
  3.7 0.0 copy-start
  3.7 1.0 copy-done
  4.7 0.0 copy-start.2
  4.7 0.7 copy-done.2
  5.4 0.0 copy-start.3
  5.4 0.7 copy-done.3
  6.1 0.0 copy-start.5
  6.1 0.7 copy-done.5
  6.8 0.0 copy-start.7
  6.8 0.7 copy-done.7
  7.4 0.5 dispatch.1
  7.9 25.7 %all_to_all.20 = bf16[8,24,1536]{2,1,0:T(8,128)(2,1)S(1)} all-to-all(bf16[8,24,1536]{2,1,0:T(8,128)(2,1)S(1)} %bitcast.22), channel_id=1, replica_groups=mesh['y'=4,'z'=8,'x'=4,'tensor'=2] {'z'}, dimensions={0} | all-to-all | bytes 1179648 | tf_op jit(solution)/shard_map/all_to_all | solution.py:168
  33.6 0.3 regroup.1
  33.9 24.3 %all_to_all.21 = bf16[16,24,1536]{2,1,0:T(8,128)(2,1)} all-to-all(bf16[16,24,1536]{2,1,0:T(8,128)(2,1)S(1)} %bitcast.18), channel_id=1, replica_groups=mesh['y'=4,'z'=8,'x'=4,'tensor'=2] {'y','x'}, dimensions={0} | all-to-all | bytes 2359296 | tf_op jit(solution)/shard_map/all_to_all | solution.py:172
  58.2 0.0 collective-permute-done
  58.2 0.0 collective-permute-done.1
  58.2 0.0 collective-permute-done.2
  58.2 12.5 %experts.1 = bf16[384,1536]{1,0:T(8,128)(2,1)} custom-call(bf16[384,1536]{1,0:T(8,128)(2,1)} %bitcast.30, bf16[1536,1024]{1,0:T(8,128)(2,1)} %bitcast.32, bf16[1536,1024]{1,0:T(8,128)(2,1)} %bitcast.33, bf16[1024,1536]{1,0:T(8,128)(2,1)} %bitcast.34, bf16[1536,1024]{1,0:T(8,128)(2,1)} %bitcast.11.refs_3_, bf16[1536,1024]{1,0:T(8,128)(2,1)} %bitcast.12.refs_4_, ...), custom_call_target="tpu_custom_call" | custom-call | flops 7247757312 | bytes 20000000 | tf_op jit(solution)/shard_map/experts/pallas_call | solution.py:201
  70.7 0.0 copy-start.4
  70.7 0.0 copy-start.6
  70.7 0.0 copy-start.8
  70.7 0.0 copy-start.9
  70.7 20.9 %all_to_all.22 = bf16[16,24,1536]{2,1,0:T(8,128)(2,1)S(1)} all-to-all(bf16[16,24,1536]{2,1,0:T(8,128)(2,1)} %bitcast.31), channel_id=1, replica_groups=mesh['y'=4,'z'=8,'x'=4,'tensor'=2] {'y','x'}, dimensions={0} | all-to-all | bytes 2359296 | tf_op jit(solution)/shard_map/all_to_all | solution.py:172
  91.6 1.3 %gather.1 = bf16[192,1536]{1,0:T(8,128)(2,1)} custom-call(bf16[384,1536]{1,0:T(8,128)(2,1)S(1)} %bitcast.19), custom_call_target="tpu_custom_call" | custom-call | tf_op jit(solution)/shard_map/gather/pallas_call | solution.py:220
  92.9 3.5 %all-to-all-start.3 = ((bf16[8,24,1536]{2,1,0:T(8,128)(2,1)}), bf16[8,24,1536]{2,1,0:T(8,128)(2,1)S(1)}, u32[]{:S(2)}, u32[]{:S(2)}) async-start(bf16[8,24,1536]{2,1,0:T(8,128)(2,1)} %bitcast.16), calls=%async_computation.3 | async-start | bytes 1179648 | tf_op jit(solution)/shard_map/all_to_all | solution.py:168
  96.5 0.0 copy-done.4
  96.5 0.0 copy-done.6
  96.5 0.0 copy-done.8
  96.5 0.0 copy-done.9
  96.5 0.0 copy-start.1
  96.5 0.4 weights.1.table
  96.9 16.2 %all-to-all-done.3 = bf16[8,24,1536]{2,1,0:T(8,128)(2,1)S(1)} async-done(((bf16[8,24,1536]{2,1,0:T(8,128)(2,1)}), bf16[8,24,1536]{2,1,0:T(8,128)(2,1)S(1)}, u32[]{:S(2)}, u32[]{:S(2)}) %all-to-all-start.3) | async-done | bytes 589856 | tf_op jit(solution)/shard_map/all_to_all | solution.py:168
  113.1 0.4 combine.1
  113.5 3.2 %collective-permute-start.3 = (bf16[128,1536]{1,0:T(8,128)(2,1)S(1)}, bf16[128,1536]{1,0:T(8,128)(2,1)S(1)}, u32[]{:S(2)}, u32[]{:S(2)}) collective-permute-start(bf16[128,1536]{1,0:T(8,128)(2,1)S(1)} %combine.1), channel_id=1, source_target_pairs={{0,1},{1,0},{2,3},{3,2},{4,5},{5,4},{6,7},{7,6},{8,9},{9,8},{10,11... | collective-permute-start | bytes 1179656 | tf_op jit(solution)/shard_map/ppermute | solution.py:20
  116.7 1.3 %collective-permute-done.3 = bf16[128,1536]{1,0:T(8,128)(2,1)S(1)} collective-permute-done((bf16[128,1536]{1,0:T(8,128)(2,1)S(1)}, bf16[128,1536]{1,0:T(8,128)(2,1)S(1)}, u32[]{:S(2)}, u32[]{:S(2)}) %collective-permute-start.3) | collective-permute-done | bytes 393248 | tf_op jit(solution)/shard_map/ppermute | solution.py:20
  118.0 0.0 copy-done.1
  118.0 0.9 add_convert_fusion
Async XLA Ops:
  0.0 58.2 %collective-permute-start = (bf16[1,1536,1024]{2,1,0:T(8,128)(2,1)}, bf16[1,1536,1024]{2,1,0:T(8,128)(2,1)}, u32[]{:S(2)}, u32[]{:S(2)}) collective-permute-start(bf16[1,1536,1024]{2,1,0:T(8,128)(2,1)} %param.12), channel_id=1, source_target_pairs={{0,1},{1,0},{2,3},{3,2},{4,5},{5,4},{6,7},{7,6},{8,9},{9,8},{10,11... | collective-permute-start | bytes 9437192 | tf_op jit(solution)/shard_map/ppermute | solution.py:20
  3.2 55.0 %collective-permute-start.1 = (bf16[1,1536,1024]{2,1,0:T(8,128)(2,1)}, bf16[1,1536,1024]{2,1,0:T(8,128)(2,1)}, u32[]{:S(2)}, u32[]{:S(2)}) collective-permute-start(bf16[1,1536,1024]{2,1,0:T(8,128)(2,1)} %param.13), channel_id=1, source_target_pairs={{0,1},{1,0},{2,3},{3,2},{4,5},{5,4},{6,7},{7,6},{8,9},{9,8},{10,11... | collective-permute-start | bytes 9437192 | tf_op jit(solution)/shard_map/ppermute | solution.py:20
  3.2 55.0 %collective-permute-start.2 = (bf16[1,1024,1536]{2,1,0:T(8,128)(2,1)}, bf16[1,1024,1536]{2,1,0:T(8,128)(2,1)}, u32[]{:S(2)}, u32[]{:S(2)}) collective-permute-start(bf16[1,1024,1536]{2,1,0:T(8,128)(2,1)} %param.14), channel_id=1, source_target_pairs={{0,1},{1,0},{2,3},{3,2},{4,5},{5,4},{6,7},{7,6},{8,9},{9,8},{10,11... | collective-permute-start | bytes 9437192 | tf_op jit(solution)/shard_map/ppermute | solution.py:20
  3.7 1.0 copy-start
  4.7 0.7 copy-start.2
  5.4 0.7 copy-start.3
  6.1 0.7 copy-start.5
  6.8 0.7 copy-start.7
  70.7 25.8 %copy-start.4 = (s32[128,2]{0,1:T(2,128)S(1)}, s32[128,2]{0,1:T(2,128)}, u32[]{:S(2)}) copy-start(s32[128,2]{0,1:T(2,128)} %param.15) | copy-start | bytes 3076
  70.7 25.8 %copy-start.6 = (s32[128,2]{0,1:T(2,128)S(1)}, s32[128,2]{0,1:T(2,128)}, u32[]{:S(2)}) copy-start(s32[128,2]{0,1:T(2,128)} %param.16) | copy-start | bytes 3076
  70.7 25.8 %copy-start.8 = (s32[128,2]{0,1:T(2,128)S(1)}, s32[128,2]{0,1:T(2,128)}, u32[]{:S(2)}) copy-start(s32[128,2]{0,1:T(2,128)} %param.17) | copy-start | bytes 3076
  70.7 25.8 %copy-start.9 = (bf16[1536,64]{0,1:T(8,128)(2,1)S(1)}, bf16[1536,64]{0,1:T(8,128)(2,1)}, u32[]{:S(2)}) copy-start(bf16[1536,64]{0,1:T(8,128)(2,1)} %param.11) | copy-start | bytes 589828
  92.9 20.2 %all-to-all-start.3 = ((bf16[8,24,1536]{2,1,0:T(8,128)(2,1)}), bf16[8,24,1536]{2,1,0:T(8,128)(2,1)S(1)}, u32[]{:S(2)}, u32[]{:S(2)}) async-start(bf16[8,24,1536]{2,1,0:T(8,128)(2,1)} %bitcast.16), calls=%async_computation.3 | async-start | bytes 1179648 | tf_op jit(solution)/shard_map/all_to_all | solution.py:168
  96.5 21.5 %copy-start.1 = (bf16[128,1536]{1,0:T(8,128)(2,1)S(1)}, bf16[128,1536]{1,0:T(8,128)(2,1)}, u32[]{:S(2)}) copy-start(bf16[128,1536]{1,0:T(8,128)(2,1)} %states.1) | copy-start | bytes 1179652
  113.5 4.5 %collective-permute-start.3 = (bf16[128,1536]{1,0:T(8,128)(2,1)S(1)}, bf16[128,1536]{1,0:T(8,128)(2,1)S(1)}, u32[]{:S(2)}, u32[]{:S(2)}) collective-permute-start(bf16[128,1536]{1,0:T(8,128)(2,1)S(1)} %combine.1), channel_id=1, source_target_pairs={{0,1},{1,0},{2,3},{3,2},{4,5},{5,4},{6,7},{7,6},{8,9},{9,8},{10,11... | collective-permute-start | bytes 1179656 | tf_op jit(solution)/shard_map/ppermute | solution.py:20

commit v4 on v3

v4 whole, which is shorter than its diff:
```python
import functools

import jax
import jax.numpy as jnp
from jax import lax
from jax.experimental import pallas as pl
from jax.experimental.pallas import tpu as pltpu
from jax.sharding import Mesh, PartitionSpec as P

SWAP = ((0, 1), (1, 0))
AXES = (4, 8, 4)
MIB = 1 << 20
BF16 = jnp.bfloat16
F32 = jnp.float32
VMEM = pl.BlockSpec(memory_space=pltpu.VMEM)
ANY = pl.BlockSpec(memory_space=pl.ANY)


def swap(x):
    return lax.ppermute(x, "tensor", SWAP)


def dot(a, b):
    return jnp.dot(a, b, preferred_element_type=F32)


def iota(shape, dim):
    return lax.broadcasted_iota(jnp.int32, shape, dim)


def slot_keys(own, tokens):
    ys, zs, xs = AXES
    pairs = xs // 2
    shape = (zs, own, ys * pairs, tokens)
    inner = iota(shape, 2)
    expert = (inner // pairs * zs + iota(shape, 0)) * pairs + inner % pairs
    key = expert * (2 * own) + iota(shape, 1) + lax.axis_index("tensor") * own
    return key.reshape(zs * own * ys * pairs, tokens)


def slot_numbers(own, ids, pos, keep):
    return jnp.where(keep[...] > 0, ids[...] * (2 * own) + pos[...], -1)


def dispatch_kernel(own, *refs):
    sources, (normed_out, send), targets, sems = refs[:5], refs[5:7], refs[7:12], refs[12]
    copies = [
        pltpu.make_async_copy(source, target, sems.at[n])
        for n, (source, target) in enumerate(zip(sources, targets))
    ]
    for copy in copies:
        copy.start()
    states, gain, ids, pos, keep = targets
    tokens = states.shape[0]
    for copy in copies[2:]:
        copy.wait()
    slots = slot_numbers(own, ids, pos, keep)
    key = slot_keys(own, tokens)
    hit = (key == slots[0:1, :]) | (key == slots[1:2, :])
    pick = jnp.where(hit, 1.0, 0.0).astype(BF16)
    for copy in copies[:2]:
        copy.wait()
    values = states[...].astype(F32)
    mean = jnp.mean(values * values, axis=-1, keepdims=True)
    normed = (values * lax.rsqrt(mean + 1e-06) * gain[...][None, :]).astype(BF16)
    normed_out[...] = normed
    send[...] = dot(pick, normed).astype(BF16)


def regroup_kernel(own, arrived, send):
    ys, zs, xs = AXES
    experts = ys * xs // 2
    count = experts * own * zs
    shape = (experts, own, zs, count)
    source = (iota(shape, 2) * own + iota(shape, 1)) * experts + iota(shape, 0)
    pick = (source == iota(shape, 3)).reshape(count, count)
    rows = dot(jnp.where(pick, 1.0, 0.0).astype(BF16), arrived[...]).astype(BF16)
    size = own * zs
    for e in range(experts):
        for h in range(2):
            send[(2 * e + h) * size : (2 * e + h + 1) * size, :] = rows[e * size : (e + 1) * size, :]


def gather_kernel(own, partial, send):
    ys, zs, xs = AXES
    experts = ys * xs // 2
    count = experts * own * zs
    shape = (zs, own, experts, 2 * count)
    holder = (iota(shape, 2) * 2 * own + iota(shape, 1)) * zs + iota(shape, 0)
    column = iota(shape, 3)
    pick = ((column == holder) | (column == holder + own * zs)).reshape(count, 2 * count)
    send[...] = dot(jnp.where(pick, 1.0, 0.0).astype(BF16), partial[...]).astype(BF16)


def weigh(own, normed, router, ids, pos, keep, table):
    tokens = normed.shape[0]
    experts = router.shape[0]
    logits = lax.dot_general(
        router[...], normed[...], (((1,), (1,)), ((), ())), preferred_element_type=F32
    )
    expert = iota((experts, tokens), 0)
    score = []
    for k in range(2):
        chosen = jnp.sum(jnp.where(expert == ids[k : k + 1, :], logits, 0.0), axis=0, keepdims=True)
        score.append(1.0 / (1.0 + jnp.exp(-chosen)))
    total = score[0] + score[1]
    slots = slot_numbers(own, ids, pos, keep)
    key = slot_keys(own, tokens)
    share = jnp.where(key == slots[0:1, :], score[0] / total, 0.0)
    share = share + jnp.where(key == slots[1:2, :], score[1] / total, 0.0)
    share = share.T
    high = share.astype(BF16)
    table[0] = high
    table[1] = (share - high.astype(F32)).astype(BF16)


def expert_kernel(own, rows, *refs):
    theirs, gate_mine, distant, routing = refs[:3], refs[3], refs[4:6], refs[6:11]
    back, table, hidden, up_mine, down_mine, sems = refs[11:]
    width = rows.shape[1]
    part = gate_mine.shape[1]
    block = 512
    copies = [
        pltpu.make_async_copy(source, target, sems.at[n])
        for n, (source, target) in enumerate(zip(distant, (up_mine, down_mine)))
    ]
    for copy in copies:
        copy.start()
    weigh(own, *routing, table)

    def hide(gates, ups, at):
        for n in range(part // block):
            cols = slice(n * block, (n + 1) * block)
            gate = dot(rows[...], gates[:, cols])
            up = dot(rows[...], ups[:, cols])
            hidden[:, at + n * block : at + (n + 1) * block] = (
                gate / (1.0 + jnp.exp(-gate)) * up
            ).astype(BF16)

    hide(theirs[0], theirs[1], 0)
    copies[0].wait()
    hide(gate_mine, up_mine, part)
    copies[1].wait()
    for n in range(width // block):
        cols = slice(n * block, (n + 1) * block)
        total = dot(hidden[:, :part], theirs[2][:, cols])
        total = total + dot(hidden[:, part:], down_mine[:, cols])
        back[:, cols] = total.astype(BF16)


def combine_kernel(table, returned, partial):
    partial[...] = (dot(table[0], returned[...]) + dot(table[1], returned[...])).astype(BF16)


def near(x):
    return pltpu.with_memory_space_constraint(x, pltpu.VMEM)


def far(x):
    return pltpu.with_memory_space_constraint(x, pltpu.HBM)


def params(mib):
    return pltpu.CompilerParams(vmem_limit_bytes=mib * MIB)


def per_device(states, norm_gain, router, w_gate, w_up, w_down, expert_ids, slot_pos, keep_mask):
    tokens, width = states.shape
    ys, zs, xs = AXES
    experts = router.shape[1]
    own = max(2, 5 * tokens // (2 * experts) + 1) // 2
    part = w_gate.shape[2]
    chips = ys * xs
    once = own * experts
    rows = pltpu.VMEM((once, width), BF16)
    twice = pltpu.VMEM((2 * once, width), BF16)
    mine = (w_gate[0], w_up[0], w_down[0])
    theirs = tuple(swap(w)[0] for w in (w_gate, w_up, w_down))
    routing = (expert_ids.T, slot_pos.T, keep_mask.T)

    def along_z(x):
        x = x.reshape(zs, once // zs, width)
        return near(lax.all_to_all(x, "z", 0, 0, tiled=True).reshape(once, width))

    def in_plane(x):
        x = x.reshape(chips, 2 * once // chips, width)
        x = lax.all_to_all(x, ("y", "x"), 0, 0, tiled=True)
        return near(x.reshape(2 * once, width))

    loaded = (states, norm_gain, *routing)
    normed, send = pl.pallas_call(
        functools.partial(dispatch_kernel, own),
        out_shape=(pltpu.VMEM(states.shape, BF16), rows),
        in_specs=[ANY] * 5,
        out_specs=(VMEM, VMEM),
        scratch_shapes=[pltpu.VMEM(x.shape, x.dtype) for x in loaded]
        + [pltpu.SemaphoreType.DMA((5,))],
        compiler_params=params(16),
        name="dispatch",
    )(*map(far, loaded))
    spread = pl.pallas_call(
        functools.partial(regroup_kernel, own),
        out_shape=twice,
        in_specs=[VMEM],
        out_specs=VMEM,
        compiler_params=params(16),
        name="regroup",
    )(along_z(send))
    back, table = pl.pallas_call(
        functools.partial(expert_kernel, own),
        out_shape=(twice, pltpu.VMEM((2, tokens, once), BF16)),
        in_specs=[VMEM] * 5 + [ANY] * 2 + [VMEM] * 5,
        out_specs=(VMEM, VMEM),
        scratch_shapes=[
            pltpu.VMEM((2 * once, 2 * part), BF16),
            pltpu.VMEM((width, part), BF16),
            pltpu.VMEM((part, width), BF16),
            pltpu.SemaphoreType.DMA((2,)),
        ],
        compiler_params=params(40),
        cost_estimate=pl.CostEstimate(
            flops=24 * once * width * part, bytes_accessed=20 * 10**6, transcendentals=0
        ),
        name="experts",
    )(
        in_plane(spread),
        *map(near, theirs + mine[:1]),
        *map(far, mine[1:]),
        near(normed),
        router.T,
        *routing,
    )
    summed = pl.pallas_call(
        functools.partial(gather_kernel, own),
        out_shape=rows,
        in_specs=[VMEM],
        out_specs=VMEM,
        compiler_params=params(16),
        name="gather",
    )(in_plane(back))
    partial = pl.pallas_call(
        combine_kernel,
        out_shape=pltpu.VMEM(states.shape, BF16),
        in_specs=[VMEM, VMEM],
        out_specs=VMEM,
        compiler_params=params(16),
        name="combine",
    )(near(table), along_z(summed))
    added = partial.astype(F32) + swap(partial).astype(F32)
    return (states.astype(F32) + added).astype(BF16)


def solution(mesh):
    grid = Mesh(mesh.devices.reshape(*AXES, 2), ("y", "z", "x", "tensor"))
    group = ("y", "z", "x")
    placed = (
        P(group, None),
        P(),
        P(),
        P(group, None, "tensor"),
        P(group, None, "tensor"),
        P(group, "tensor", None),
        P(group, None),
        P(group, None),
        P(group, None),
    )
    return jax.shard_map(
        per_device, mesh=grid, in_specs=placed, out_specs=P(group, None), check_vma=False
    )
```

time: 119 us -> 108 us (0.908)
  waiting for transfers between devices: 17.6 us -> 1.36 us
  blocking collectives: 70.9 us -> 85.1 us
  local copies, waits for them, and re-layouts: 3.76 us -> 0.01 us
  Pallas kernels: 15.3 us -> 11.6 us
  starting transfers between devices: 10.4 us -> 9.03 us
    all_to_all x1 -> x0, waiting for transfers between devices: 16.2 us -> none  [along_z(): return lax.all_to_all(x, 'z', 0, 0, tiled=True).reshape(once, width)]
    all_to_all x3 -> x4, blocking collectives: 70.9 us -> 85.1 us  [the longest x2 42.7 us: along_z(): return near(lax.all_to_all(x, 'z', 0, 0, tiled=True).reshape(once, width))]
    unnamed x20 -> x4, local copies, waits for them, and re-layouts: 3.76 us -> 0.01 us
    all_to_all x1 -> x0, starting transfers between devices: 3.54 us -> none  [along_z(): return lax.all_to_all(x, 'z', 0, 0, tiled=True).reshape(once, width)]
    pallas_call x4 -> x3, Pallas kernels: 13.7 us -> 10.8 us  [the longest x1 8.97 us: per_device(): pl.pallas_call(functools.partial(expert_kernel, own), out_shape=(twice, p...]
    ppermute x4, starting transfers between devices: 6.89 us -> 9.03 us  [swap(): return lax.ppermute(x, 'tensor', SWAP)]
  transfers between devices with their start and end apart: 5 -> 4, of which waited for: 2 -> 1; matrix products, arithmetic and copies ran while one was open for 0% -> 0% of each run, Pallas kernels for 1% -> 2%
where the time goes in v4:
time: 108 us
  blocking collectives  85.1 us (79%)
  Pallas kernels  11.6 us (11%)
  starting transfers between devices  9.03 us (8%)
  waiting for transfers between devices  1.36 us (1%)
    all_to_all x2, blocking collectives, along_z(): return near(lax.all_to_all(x, 'z', 0, 0, tiled=True).reshape(once, width))  42.7 us
    all_to_all x2, blocking collectives, in_plane(): x = lax.all_to_all(x, ('y', 'x'), 0, 0, tiled=True)  42.4 us
    ppermute x4, starting transfers between devices, swap(): return lax.ppermute(x, 'tensor', SWAP)  9.03 us
    pallas_call x1, Pallas kernels, per_device(): pl.pallas_call(functools.partial(expert_kernel, own), out_shape=(twice, p...  8.97 us
  transfers between devices with their start and end apart: 4, of which 1 were waited for; matrix products, arithmetic and copies ran while one was open for 0% of the time, Pallas kernels for 2%

profile of v4, /device:TPU:1, one launch (start us, length us, event | category | flops | bytes accessed | tf_op | source)
XLA Modules:
  0.0 108.1 jit_solution(12755700838488359585)
XLA Ops:
  0.0 0.0 copy-start
  0.0 3.2 %collective-permute-start = (bf16[1,1536,1024]{2,1,0:T(8,128)(2,1)}, bf16[1,1536,1024]{2,1,0:T(8,128)(2,1)S(1)}, u32[]{:S(2)}, u32[]{:S(2)}) collective-permute-start(bf16[1,1536,1024]{2,1,0:T(8,128)(2,1)} %param.12), channel_id=1, source_target_pairs={{0,1},{1,0},{2,3},{3,2},{4,5},{5,4},{6,7},{7,6},{8,9},{9,8},{10,11... | collective-permute-start | bytes 9437192 | tf_op jit(solution)/shard_map/ppermute | solution.py:20
  3.2 0.0 collective-permute-start.1
  3.2 0.5 collective-permute-start.2
  3.7 1.5 %dispatch.1 = (bf16[128,1536]{1,0:T(8,128)(2,1)S(1)}, bf16[192,1536]{1,0:T(8,128)(2,1)S(1)}) custom-call(bf16[128,1536]{1,0:T(8,128)(2,1)} %refs_0_.1, f32[1536]{0:T(1024)} %refs_1_.1, s32[2,128]{1,0:T(2,128)} %bitcast.30, s32[2,128]{1,0:T(2,128)} %bitcast.32, s32[2,128]{1,0:T(2,128)} %bitcast.34), custom_call_target="tpu_custom_call" | custom-call | tf_op jit(solution)/shard_map/dispatch/pallas_call | solution.py:191
  5.2 24.7 %all_to_all.20 = bf16[8,24,1536]{2,1,0:T(8,128)(2,1)S(1)} all-to-all(bf16[8,24,1536]{2,1,0:T(8,128)(2,1)S(1)} %bitcast.25), channel_id=1, replica_groups=mesh['y'=4,'z'=8,'x'=4,'tensor'=2] {'z'}, dimensions={0} | all-to-all | bytes 1179648 | tf_op jit(solution)/shard_map/all_to_all | solution.py:183
  29.9 0.3 regroup.1
  30.2 23.6 %all_to_all.21 = bf16[16,24,1536]{2,1,0:T(8,128)(2,1)S(1)} all-to-all(bf16[16,24,1536]{2,1,0:T(8,128)(2,1)S(1)} %bitcast.18), channel_id=1, replica_groups=mesh['y'=4,'z'=8,'x'=4,'tensor'=2] {'y','x'}, dimensions={0} | all-to-all | bytes 2359296 | tf_op jit(solution)/shard_map/all_to_all | solution.py:187
  53.8 0.0 collective-permute-done
  53.8 0.0 collective-permute-done.1
  53.8 0.0 collective-permute-done.2
  53.8 0.0 copy-done
  53.8 9.0 %experts.1 = (bf16[384,1536]{1,0:T(8,128)(2,1)S(1)}, bf16[2,128,192]{2,1,0:T(8,128)(2,1)S(1)}) custom-call(bf16[384,1536]{1,0:T(8,128)(2,1)S(1)} %bitcast.23, bf16[1536,1024]{1,0:T(8,128)(2,1)S(1)} %bitcast.27, bf16[1536,1024]{1,0:T(8,128)(2,1)S(1)} %bitcast.28, bf16[1024,1536]{1,0:T(8,128)(2,1)S(1)} %bitcast.29, bf16[1536,1024]{1,0:T(8,128)(2,1)S(1)} %bitcast.26, ...), custom_call_target="tpu_custom_call" | custom-call | flops 7247757312 | bytes 20000000 | tf_op jit(solution)/shard_map/experts/pallas_call | solution.py:209
  62.8 0.0 copy-start.1
  62.8 18.9 %all_to_all.22 = bf16[16,24,1536]{2,1,0:T(8,128)(2,1)S(1)} all-to-all(bf16[16,24,1536]{2,1,0:T(8,128)(2,1)S(1)} %bitcast.24), channel_id=1, replica_groups=mesh['y'=4,'z'=8,'x'=4,'tensor'=2] {'y','x'}, dimensions={0} | all-to-all | bytes 2359296 | tf_op jit(solution)/shard_map/all_to_all | solution.py:187
  81.6 0.5 gather.1
  82.1 18.0 %all_to_all.23 = bf16[8,24,1536]{2,1,0:T(8,128)(2,1)S(1)} all-to-all(bf16[8,24,1536]{2,1,0:T(8,128)(2,1)S(1)} %bitcast.21), channel_id=1, replica_groups=mesh['y'=4,'z'=8,'x'=4,'tensor'=2] {'z'}, dimensions={0} | all-to-all | bytes 1179648 | tf_op jit(solution)/shard_map/all_to_all | solution.py:183
  100.2 0.4 combine.1
  100.5 5.3 %collective-permute-start.3 = (bf16[128,1536]{1,0:T(8,128)(2,1)S(1)}, bf16[128,1536]{1,0:T(8,128)(2,1)S(1)}, u32[]{:S(2)}, u32[]{:S(2)}) collective-permute-start(bf16[128,1536]{1,0:T(8,128)(2,1)S(1)} %combine.1), channel_id=1, source_target_pairs={{0,1},{1,0},{2,3},{3,2},{4,5},{5,4},{6,7},{7,6},{8,9},{9,8},{10,11... | collective-permute-start | bytes 1179656 | tf_op jit(solution)/shard_map/ppermute | solution.py:20
  105.9 1.3 %collective-permute-done.3 = bf16[128,1536]{1,0:T(8,128)(2,1)S(1)} collective-permute-done((bf16[128,1536]{1,0:T(8,128)(2,1)S(1)}, bf16[128,1536]{1,0:T(8,128)(2,1)S(1)}, u32[]{:S(2)}, u32[]{:S(2)}) %collective-permute-start.3) | collective-permute-done | bytes 393248 | tf_op jit(solution)/shard_map/ppermute | solution.py:20
  107.2 0.0 copy-done.1
  107.2 0.9 add_convert_fusion
Async XLA Ops:
  0.0 53.8 %copy-start = (bf16[1,1536,1024]{2,1,0:T(8,128)(2,1)S(1)}, bf16[1,1536,1024]{2,1,0:T(8,128)(2,1)}, u32[]{:S(2)}) copy-start(bf16[1,1536,1024]{2,1,0:T(8,128)(2,1)} %param.12) | copy-start | bytes 9437188
  0.0 53.8 %collective-permute-start = (bf16[1,1536,1024]{2,1,0:T(8,128)(2,1)}, bf16[1,1536,1024]{2,1,0:T(8,128)(2,1)S(1)}, u32[]{:S(2)}, u32[]{:S(2)}) collective-permute-start(bf16[1,1536,1024]{2,1,0:T(8,128)(2,1)} %param.12), channel_id=1, source_target_pairs={{0,1},{1,0},{2,3},{3,2},{4,5},{5,4},{6,7},{7,6},{8,9},{9,8},{10,11... | collective-permute-start | bytes 9437192 | tf_op jit(solution)/shard_map/ppermute | solution.py:20
  3.2 50.6 %collective-permute-start.1 = (bf16[1,1536,1024]{2,1,0:T(8,128)(2,1)}, bf16[1,1536,1024]{2,1,0:T(8,128)(2,1)S(1)}, u32[]{:S(2)}, u32[]{:S(2)}) collective-permute-start(bf16[1,1536,1024]{2,1,0:T(8,128)(2,1)} %param.13), channel_id=1, source_target_pairs={{0,1},{1,0},{2,3},{3,2},{4,5},{5,4},{6,7},{7,6},{8,9},{9,8},{10,11... | collective-permute-start | bytes 9437192 | tf_op jit(solution)/shard_map/ppermute | solution.py:20
  3.2 50.6 %collective-permute-start.2 = (bf16[1,1024,1536]{2,1,0:T(8,128)(2,1)}, bf16[1,1024,1536]{2,1,0:T(8,128)(2,1)S(1)}, u32[]{:S(2)}, u32[]{:S(2)}) collective-permute-start(bf16[1,1024,1536]{2,1,0:T(8,128)(2,1)} %param.14), channel_id=1, source_target_pairs={{0,1},{1,0},{2,3},{3,2},{4,5},{5,4},{6,7},{7,6},{8,9},{9,8},{10,11... | collective-permute-start | bytes 9437192 | tf_op jit(solution)/shard_map/ppermute | solution.py:20
  62.8 44.4 %copy-start.1 = (bf16[128,1536]{1,0:T(8,128)(2,1)S(1)}, bf16[128,1536]{1,0:T(8,128)(2,1)}, u32[]{:S(2)}) copy-start(bf16[128,1536]{1,0:T(8,128)(2,1)} %refs_0_.1) | copy-start | bytes 1179652
  100.5 6.7 %collective-permute-start.3 = (bf16[128,1536]{1,0:T(8,128)(2,1)S(1)}, bf16[128,1536]{1,0:T(8,128)(2,1)S(1)}, u32[]{:S(2)}, u32[]{:S(2)}) collective-permute-start(bf16[128,1536]{1,0:T(8,128)(2,1)S(1)} %combine.1), channel_id=1, source_target_pairs={{0,1},{1,0},{2,3},{3,2},{4,5},{5,4},{6,7},{7,6},{8,9},{9,8},{10,11... | collective-permute-start | bytes 1179656 | tf_op jit(solution)/shard_map/ppermute | solution.py:20

commit v5 on v4

--- a/solution.py
+++ b/solution.py
@@ -2,13 +2,16 @@
 
 import jax
 import jax.numpy as jnp
+import numpy as np
 from jax import lax
 from jax.experimental import pallas as pl
 from jax.experimental.pallas import tpu as pltpu
-from jax.sharding import Mesh, PartitionSpec as P
+from jax.sharding import PartitionSpec as P
+
 
 SWAP = ((0, 1), (1, 0))
 AXES = (4, 8, 4)
+SIDE = 8
 MIB = 1 << 20
 BF16 = jnp.bfloat16
 F32 = jnp.float32
@@ -29,13 +32,30 @@
 
 
 def slot_keys(own, tokens):
+    _, zs, xs = AXES
+    pairs = xs // 2
+    core = lax.axis_index("tensor")
+    shape = (SIDE, own, SIDE, tokens)
+    outer, inner = iota(shape, 0), iota(shape, 2)
+    z = jnp.where(core == 0, outer, inner)
+    plane = jnp.where(core == 0, inner, outer)
+    expert = (plane // pairs * zs + z) * pairs + plane % pairs
+    key = expert * (2 * own) + iota(shape, 1) + core * own
+    return key.reshape(SIDE * own * SIDE, tokens)
+
+
+def stage_groups():
     ys, zs, xs = AXES
-    pairs = xs // 2
-    shape = (zs, own, ys * pairs, tokens)
-    inner = iota(shape, 2)
-    expert = (inner // pairs * zs + iota(shape, 0)) * pairs + inner % pairs
-    key = expert * (2 * own) + iota(shape, 1) + lax.axis_index("tensor") * own
-    return key.reshape(zs * own * ys * pairs, tokens)
+    flat = np.arange(ys * zs * xs * 2).reshape(ys, zs, xs // 2, 2, 2)
+    first = (
+        flat[..., 0].transpose(0, 2, 3, 1).reshape(-1, zs),
+        flat[..., 1].transpose(1, 3, 0, 2).reshape(-1, ys * xs // 2),
+    )
+    second = (
+        flat[..., 0].transpose(1, 0, 2, 3).reshape(-1, ys * xs),
+        flat[..., 1].transpose(0, 2, 1, 3).reshape(-1, 2 * zs),
+    )
+    return tuple(np.concatenate(part).tolist() for part in (first, second))
 
 
 def slot_numbers(own, ids, pos, keep):
@@ -68,27 +88,23 @@
 
 
 def regroup_kernel(own, arrived, send):
-    ys, zs, xs = AXES
-    experts = ys * xs // 2
-    count = experts * own * zs
-    shape = (experts, own, zs, count)
-    source = (iota(shape, 2) * own + iota(shape, 1)) * experts + iota(shape, 0)
+    count = SIDE * own * SIDE
+    shape = (SIDE, own, SIDE, count)
+    source = (iota(shape, 2) * own + iota(shape, 1)) * SIDE + iota(shape, 0)
     pick = (source == iota(shape, 3)).reshape(count, count)
     rows = dot(jnp.where(pick, 1.0, 0.0).astype(BF16), arrived[...]).astype(BF16)
-    size = own * zs
-    for e in range(experts):
+    size = own * SIDE
+    for e in range(SIDE):
         for h in range(2):
             send[(2 * e + h) * size : (2 * e + h + 1) * size, :] = rows[e * size : (e + 1) * size, :]
 
 
 def gather_kernel(own, partial, send):
-    ys, zs, xs = AXES
-    experts = ys * xs // 2
-    count = experts * own * zs
-    shape = (zs, own, experts, 2 * count)
-    holder = (iota(shape, 2) * 2 * own + iota(shape, 1)) * zs + iota(shape, 0)
+    count = SIDE * own * SIDE
+    shape = (SIDE, own, SIDE, 2 * count)
+    holder = (iota(shape, 2) * 2 * own + iota(shape, 1)) * SIDE + iota(shape, 0)
     column = iota(shape, 3)
-    pick = ((column == holder) | (column == holder + own * zs)).reshape(count, 2 * count)
+    pick = ((column == holder) | (column == holder + own * SIDE)).reshape(count, 2 * count)
     send[...] = dot(jnp.where(pick, 1.0, 0.0).astype(BF16), partial[...]).astype(BF16)
 
 
@@ -166,26 +182,26 @@
 
 def per_device(states, norm_gain, router, w_gate, w_up, w_down, expert_ids, slot_pos, keep_mask):
     tokens, width = states.shape
-    ys, zs, xs = AXES
     experts = router.shape[1]
     own = max(2, 5 * tokens // (2 * experts) + 1) // 2
     part = w_gate.shape[2]
-    chips = ys * xs
     once = own * experts
     rows = pltpu.VMEM((once, width), BF16)
     twice = pltpu.VMEM((2 * once, width), BF16)
     mine = (w_gate[0], w_up[0], w_down[0])
-    theirs = tuple(swap(w)[0] for w in (w_gate, w_up, w_down))
+    theirs = []
+    for w in (w_gate, w_up, w_down):
+        theirs.append(swap(w)[0])
     routing = (expert_ids.T, slot_pos.T, keep_mask.T)
 
-    def along_z(x):
-        x = x.reshape(zs, once // zs, width)
-        return near(lax.all_to_all(x, "z", 0, 0, tiled=True).reshape(once, width))
-
-    def in_plane(x):
-        x = x.reshape(chips, 2 * once // chips, width)
-        x = lax.all_to_all(x, ("y", "x"), 0, 0, tiled=True)
-        return near(x.reshape(2 * once, width))
+    first, second = stage_groups()
+
+    def exchange(x, groups):
+        cut = x.reshape(len(groups[0]), -1, width)
+        cut = lax.all_to_all(
+            cut, ("expert", "tensor"), 0, 0, axis_index_groups=groups, tiled=True
+        )
+        return cut.reshape(x.shape)
 
     loaded = (states, norm_gain, *routing)
     normed, send = pl.pallas_call(
@@ -198,6 +214,7 @@
         compiler_params=params(16),
         name="dispatch",
     )(*map(far, loaded))
+    column, *theirs = lax.optimization_barrier((exchange(send, first), *theirs))
     spread = pl.pallas_call(
         functools.partial(regroup_kernel, own),
         out_shape=twice,
@@ -205,7 +222,7 @@
         out_specs=VMEM,
         compiler_params=params(16),
         name="regroup",
-    )(along_z(send))
+    )(near(column))
     back, table = pl.pallas_call(
         functools.partial(expert_kernel, own),
         out_shape=(twice, pltpu.VMEM((2, tokens, once), BF16)),
@@ -223,8 +240,8 @@
         ),
         name="experts",
     )(
-        in_plane(spread),
-        *map(near, theirs + mine[:1]),
+        near(exchange(spread, second)),
+        *map(near, (*theirs, mine[0])),
         *map(far, mine[1:]),
         near(normed),
         router.T,
@@ -237,7 +254,7 @@
         out_specs=VMEM,
         compiler_params=params(16),
         name="gather",
-    )(in_plane(back))
+    )(near(exchange(back, second)))
     partial = pl.pallas_call(
         combine_kernel,
         out_shape=pltpu.VMEM(states.shape, BF16),
@@ -245,25 +262,24 @@
         out_specs=VMEM,
         compiler_params=params(16),
         name="combine",
-    )(near(table), along_z(summed))
+    )(near(table), near(exchange(summed, first)))
     added = partial.astype(F32) + swap(partial).astype(F32)
     return (states.astype(F32) + added).astype(BF16)
 
 
 def solution(mesh):
-    grid = Mesh(mesh.devices.reshape(*AXES, 2), ("y", "z", "x", "tensor"))
-    group = ("y", "z", "x")
     placed = (
-        P(group, None),
+        P("expert", None),
         P(),
         P(),
-        P(group, None, "tensor"),
-        P(group, None, "tensor"),
-        P(group, "tensor", None),
-        P(group, None),
-        P(group, None),
-        P(group, None),
-    )
+        P("expert", None, "tensor"),
+        P("expert", None, "tensor"),
+        P("expert", "tensor", None),
+        P("expert", None),
+        P("expert", None),
+        P("expert", None),
+    )
+
     return jax.shard_map(
-        per_device, mesh=grid, in_specs=placed, out_specs=P(group, None), check_vma=False
-    )
+        per_device, mesh=mesh, in_specs=placed, out_specs=P("expert", None), check_vma=False
+    )

time: 108 us -> 102 us (0.944)
  blocking collectives: 85.1 us -> 77.8 us
    all_to_all x4, blocking collectives: 85.1 us -> 77.8 us  [exchange(): lax.all_to_all(cut, ('expert', 'tensor'), 0, 0, axis_index_groups=groups,...]
  transfers between devices with their start and end apart: 4 -> 4, of which waited for: 1 -> 1; matrix products, arithmetic and copies ran while one was open for 0% -> 0% of each run, Pallas kernels for 2% -> 1%
where the time goes in v5:
time: 102 us; the launch traced here: 101 us
  blocking collectives  77.8 us (76%)
  Pallas kernels  11.6 us (11%)
  starting transfers between devices  9.66 us (9%)
  waiting for transfers between devices  1.36 us (1%)
    all_to_all x4, blocking collectives, exchange(): lax.all_to_all(cut, ('expert', 'tensor'), 0, 0, axis_index_groups=groups,...  77.8 us
    ppermute x4, starting transfers between devices, swap(): return lax.ppermute(x, 'tensor', SWAP)  9.66 us
    pallas_call x1, Pallas kernels, per_device(): pl.pallas_call(functools.partial(expert_kernel, own), out_shape=(twice, p...  8.94 us
  transfers between devices with their start and end apart: 4, of which 1 were waited for; matrix products, arithmetic and copies ran while one was open for 0% of the time, Pallas kernels for 1%

profile of v5, /device:TPU:1, one launch (start us, length us, event | category | flops | bytes accessed | tf_op | source)
XLA Modules:
  0.0 101.4 jit_solution(6260986106857217834)
XLA Ops:
  0.0 0.0 copy-start
  0.0 3.2 %collective-permute-start = (bf16[1,1536,1024]{2,1,0:T(8,128)(2,1)}, bf16[1,1536,1024]{2,1,0:T(8,128)(2,1)S(1)}, u32[]{:S(2)}, u32[]{:S(2)}) collective-permute-start(bf16[1,1536,1024]{2,1,0:T(8,128)(2,1)} %param.12), channel_id=1, source_target_pairs={{0,1},{1,0},{2,3},{3,2},{4,5},{5,4},{6,7},{7,6},{8,9},{9,8},{10,11... | collective-permute-start | bytes 9437192 | tf_op jit(solution)/shard_map/ppermute | solution.py:23
  3.2 0.0 collective-permute-start.1
  3.2 0.5 collective-permute-start.2
  3.7 1.5 %dispatch.1 = (bf16[128,1536]{1,0:T(8,128)(2,1)S(1)}, bf16[192,1536]{1,0:T(8,128)(2,1)S(1)}) custom-call(bf16[128,1536]{1,0:T(8,128)(2,1)} %refs_0_.1, f32[1536]{0:T(1024)} %refs_1_.1, s32[2,128]{1,0:T(2,128)} %bitcast.30, s32[2,128]{1,0:T(2,128)} %bitcast.32, s32[2,128]{1,0:T(2,128)} %bitcast.34), custom_call_target="tpu_custom_call" | custom-call | tf_op jit(solution)/shard_map/dispatch/pallas_call | solution.py:207
  5.2 14.3 %all_to_all.20 = bf16[8,24,1536]{2,1,0:T(8,128)(2,1)S(1)} all-to-all(bf16[8,24,1536]{2,1,0:T(8,128)(2,1)S(1)} %bitcast.25), channel_id=1, replica_groups={{0,8,16,24,32,40,48,56},{2,10,18,26,34,42,50,58},{4,12,20,28,36,44,52,6..., dimensions={0} | all-to-all | bytes 1179648 | tf_op jit(solution)/shard_map/all_to_all | solution.py:201
  19.5 0.0 collective-permute-done
  19.5 0.0 collective-permute-done.1
  19.5 0.0 collective-permute-done.2
  19.5 0.3 regroup.1
  19.8 27.8 %all_to_all.21 = bf16[16,24,1536]{2,1,0:T(8,128)(2,1)S(1)} all-to-all(bf16[16,24,1536]{2,1,0:T(8,128)(2,1)S(1)} %bitcast.18), channel_id=1, replica_groups={{0,2,4,6,64,66,68,70,128,130,132,134,192,194,196,198},{8,10,12,14,72,74..., dimensions={0} | all-to-all | bytes 2359296 | tf_op jit(solution)/shard_map/all_to_all | solution.py:201
  47.6 0.0 copy-done
  47.6 8.9 %experts.1 = (bf16[384,1536]{1,0:T(8,128)(2,1)S(1)}, bf16[2,128,192]{2,1,0:T(8,128)(2,1)S(1)}) custom-call(bf16[384,1536]{1,0:T(8,128)(2,1)S(1)} %bitcast.23, bf16[1536,1024]{1,0:T(8,128)(2,1)S(1)} %bitcast.27, bf16[1536,1024]{1,0:T(8,128)(2,1)S(1)} %bitcast.28, bf16[1024,1536]{1,0:T(8,128)(2,1)S(1)} %bitcast.29, bf16[1536,1024]{1,0:T(8,128)(2,1)S(1)} %bitcast.26, ...), custom_call_target="tpu_custom_call" | custom-call | flops 7247757312 | bytes 20000000 | tf_op jit(solution)/shard_map/experts/pallas_call | solution.py:226
  56.6 0.0 copy-start.1
  56.6 22.9 %all_to_all.22 = bf16[16,24,1536]{2,1,0:T(8,128)(2,1)S(1)} all-to-all(bf16[16,24,1536]{2,1,0:T(8,128)(2,1)S(1)} %bitcast.24), channel_id=1, replica_groups={{0,2,4,6,64,66,68,70,128,130,132,134,192,194,196,198},{8,10,12,14,72,74..., dimensions={0} | all-to-all | bytes 2359296 | tf_op jit(solution)/shard_map/all_to_all | solution.py:201
  79.4 0.5 gather.1
  79.9 12.9 %all_to_all.23 = bf16[8,24,1536]{2,1,0:T(8,128)(2,1)S(1)} all-to-all(bf16[8,24,1536]{2,1,0:T(8,128)(2,1)S(1)} %bitcast.21), channel_id=1, replica_groups={{0,8,16,24,32,40,48,56},{2,10,18,26,34,42,50,58},{4,12,20,28,36,44,52,6..., dimensions={0} | all-to-all | bytes 1179648 | tf_op jit(solution)/shard_map/all_to_all | solution.py:201
  92.8 0.4 combine.1
  93.2 5.9 %collective-permute-start.3 = (bf16[128,1536]{1,0:T(8,128)(2,1)S(1)}, bf16[128,1536]{1,0:T(8,128)(2,1)S(1)}, u32[]{:S(2)}, u32[]{:S(2)}) collective-permute-start(bf16[128,1536]{1,0:T(8,128)(2,1)S(1)} %combine.1), channel_id=1, source_target_pairs={{0,1},{1,0},{2,3},{3,2},{4,5},{5,4},{6,7},{7,6},{8,9},{9,8},{10,11... | collective-permute-start | bytes 1179656 | tf_op jit(solution)/shard_map/ppermute | solution.py:23
  99.1 1.3 %collective-permute-done.3 = bf16[128,1536]{1,0:T(8,128)(2,1)S(1)} collective-permute-done((bf16[128,1536]{1,0:T(8,128)(2,1)S(1)}, bf16[128,1536]{1,0:T(8,128)(2,1)S(1)}, u32[]{:S(2)}, u32[]{:S(2)}) %collective-permute-start.3) | collective-permute-done | bytes 393248 | tf_op jit(solution)/shard_map/ppermute | solution.py:23
  100.5 0.0 copy-done.1
  100.5 0.9 add_convert_fusion
Async XLA Ops:
  0.0 47.6 %copy-start = (bf16[1,1536,1024]{2,1,0:T(8,128)(2,1)S(1)}, bf16[1,1536,1024]{2,1,0:T(8,128)(2,1)}, u32[]{:S(2)}) copy-start(bf16[1,1536,1024]{2,1,0:T(8,128)(2,1)} %param.12) | copy-start | bytes 9437188
  0.0 19.5 %collective-permute-start = (bf16[1,1536,1024]{2,1,0:T(8,128)(2,1)}, bf16[1,1536,1024]{2,1,0:T(8,128)(2,1)S(1)}, u32[]{:S(2)}, u32[]{:S(2)}) collective-permute-start(bf16[1,1536,1024]{2,1,0:T(8,128)(2,1)} %param.12), channel_id=1, source_target_pairs={{0,1},{1,0},{2,3},{3,2},{4,5},{5,4},{6,7},{7,6},{8,9},{9,8},{10,11... | collective-permute-start | bytes 9437192 | tf_op jit(solution)/shard_map/ppermute | solution.py:23
  3.2 16.3 %collective-permute-start.1 = (bf16[1,1536,1024]{2,1,0:T(8,128)(2,1)}, bf16[1,1536,1024]{2,1,0:T(8,128)(2,1)S(1)}, u32[]{:S(2)}, u32[]{:S(2)}) collective-permute-start(bf16[1,1536,1024]{2,1,0:T(8,128)(2,1)} %param.13), channel_id=1, source_target_pairs={{0,1},{1,0},{2,3},{3,2},{4,5},{5,4},{6,7},{7,6},{8,9},{9,8},{10,11... | collective-permute-start | bytes 9437192 | tf_op jit(solution)/shard_map/ppermute | solution.py:23
  3.2 16.3 %collective-permute-start.2 = (bf16[1,1024,1536]{2,1,0:T(8,128)(2,1)}, bf16[1,1024,1536]{2,1,0:T(8,128)(2,1)S(1)}, u32[]{:S(2)}, u32[]{:S(2)}) collective-permute-start(bf16[1,1024,1536]{2,1,0:T(8,128)(2,1)} %param.14), channel_id=1, source_target_pairs={{0,1},{1,0},{2,3},{3,2},{4,5},{5,4},{6,7},{7,6},{8,9},{9,8},{10,11... | collective-permute-start | bytes 9437192 | tf_op jit(solution)/shard_map/ppermute | solution.py:23
  56.6 43.9 %copy-start.1 = (bf16[128,1536]{1,0:T(8,128)(2,1)S(1)}, bf16[128,1536]{1,0:T(8,128)(2,1)}, u32[]{:S(2)}) copy-start(bf16[128,1536]{1,0:T(8,128)(2,1)} %refs_0_.1) | copy-start | bytes 1179652
  93.2 7.3 %collective-permute-start.3 = (bf16[128,1536]{1,0:T(8,128)(2,1)S(1)}, bf16[128,1536]{1,0:T(8,128)(2,1)S(1)}, u32[]{:S(2)}, u32[]{:S(2)}) collective-permute-start(bf16[128,1536]{1,0:T(8,128)(2,1)S(1)} %combine.1), channel_id=1, source_target_pairs={{0,1},{1,0},{2,3},{3,2},{4,5},{5,4},{6,7},{7,6},{8,9},{9,8},{10,11... | collective-permute-start | bytes 1179656 | tf_op jit(solution)/shard_map/ppermute | solution.py:23

commit v6 on v5

--- a/solution.py
+++ b/solution.py
@@ -37,8 +37,8 @@
     core = lax.axis_index("tensor")
     shape = (SIDE, own, SIDE, tokens)
     outer, inner = iota(shape, 0), iota(shape, 2)
-    z = jnp.where(core == 0, outer, inner)
-    plane = jnp.where(core == 0, inner, outer)
+    z = jnp.where(core == 1, outer, inner)
+    plane = jnp.where(core == 1, inner, outer)
     expert = (plane // pairs * zs + z) * pairs + plane % pairs
     key = expert * (2 * own) + iota(shape, 1) + core * own
     return key.reshape(SIDE * own * SIDE, tokens)
@@ -48,12 +48,12 @@
     ys, zs, xs = AXES
     flat = np.arange(ys * zs * xs * 2).reshape(ys, zs, xs // 2, 2, 2)
     first = (
-        flat[..., 0].transpose(0, 2, 3, 1).reshape(-1, zs),
-        flat[..., 1].transpose(1, 3, 0, 2).reshape(-1, ys * xs // 2),
+        flat[..., 1].transpose(0, 2, 3, 1).reshape(-1, zs),
+        flat[..., 0].transpose(1, 3, 0, 2).reshape(-1, ys * xs // 2),
     )
     second = (
-        flat[..., 0].transpose(1, 0, 2, 3).reshape(-1, ys * xs),
-        flat[..., 1].transpose(0, 2, 1, 3).reshape(-1, 2 * zs),
+        flat[..., 1].transpose(1, 0, 2, 3).reshape(-1, ys * xs),
+        flat[..., 0].transpose(0, 2, 1, 3).reshape(-1, 2 * zs),
     )
     return tuple(np.concatenate(part).tolist() for part in (first, second))
 

time: 102 us -> 101 us (level)
  no operation moved by 1% of the time
where the time goes in v6:
time: 101 us; the launch traced here: 100 us
  blocking collectives  77.2 us (76%)
  Pallas kernels  11.6 us (11%)
  starting transfers between devices  9.29 us (9%)
  waiting for transfers between devices  1.36 us (1%)
    all_to_all x4, blocking collectives, exchange(): lax.all_to_all(cut, ('expert', 'tensor'), 0, 0, axis_index_groups=groups,...  77.2 us
    ppermute x4, starting transfers between devices, swap(): return lax.ppermute(x, 'tensor', SWAP)  9.29 us
    pallas_call x1, Pallas kernels, per_device(): pl.pallas_call(functools.partial(expert_kernel, own), out_shape=(twice, p...  8.97 us
  transfers between devices with their start and end apart: 4, of which 1 were waited for; matrix products, arithmetic and copies ran while one was open for 0% of the time, Pallas kernels for 1%

profile of v6, /device:TPU:1, one launch (start us, length us, event | category | flops | bytes accessed | tf_op | source)
XLA Modules:
  0.0 100.4 jit_solution(17775815956878395066)
XLA Ops:
  0.0 0.0 copy-start
  0.0 3.2 %collective-permute-start = (bf16[1,1536,1024]{2,1,0:T(8,128)(2,1)}, bf16[1,1536,1024]{2,1,0:T(8,128)(2,1)S(1)}, u32[]{:S(2)}, u32[]{:S(2)}) collective-permute-start(bf16[1,1536,1024]{2,1,0:T(8,128)(2,1)} %param.12), channel_id=1, source_target_pairs={{0,1},{1,0},{2,3},{3,2},{4,5},{5,4},{6,7},{7,6},{8,9},{9,8},{10,11... | collective-permute-start | bytes 9437192 | tf_op jit(solution)/shard_map/ppermute | solution.py:23
  3.2 0.0 collective-permute-start.1
  3.2 0.5 collective-permute-start.2
  3.7 1.5 %dispatch.1 = (bf16[128,1536]{1,0:T(8,128)(2,1)S(1)}, bf16[192,1536]{1,0:T(8,128)(2,1)S(1)}) custom-call(bf16[128,1536]{1,0:T(8,128)(2,1)} %refs_0_.1, f32[1536]{0:T(1024)} %refs_1_.1, s32[2,128]{1,0:T(2,128)} %bitcast.30, s32[2,128]{1,0:T(2,128)} %bitcast.32, s32[2,128]{1,0:T(2,128)} %bitcast.34), custom_call_target="tpu_custom_call" | custom-call | tf_op jit(solution)/shard_map/dispatch/pallas_call | solution.py:207
  5.2 19.1 %all_to_all.20 = bf16[8,24,1536]{2,1,0:T(8,128)(2,1)S(1)} all-to-all(bf16[8,24,1536]{2,1,0:T(8,128)(2,1)S(1)} %bitcast.25), channel_id=1, replica_groups={{1,9,17,25,33,41,49,57},{3,11,19,27,35,43,51,59},{5,13,21,29,37,45,53,6..., dimensions={0} | all-to-all | bytes 1179648 | tf_op jit(solution)/shard_map/all_to_all | solution.py:201
  24.3 0.0 collective-permute-done
  24.3 0.0 collective-permute-done.1
  24.3 0.0 collective-permute-done.2
  24.4 0.3 regroup.1
  24.7 24.2 %all_to_all.21 = bf16[16,24,1536]{2,1,0:T(8,128)(2,1)S(1)} all-to-all(bf16[16,24,1536]{2,1,0:T(8,128)(2,1)S(1)} %bitcast.18), channel_id=1, replica_groups={{1,3,5,7,65,67,69,71,129,131,133,135,193,195,197,199},{9,11,13,15,73,75..., dimensions={0} | all-to-all | bytes 2359296 | tf_op jit(solution)/shard_map/all_to_all | solution.py:201
  48.8 0.0 copy-done
  48.8 9.0 %experts.1 = (bf16[384,1536]{1,0:T(8,128)(2,1)S(1)}, bf16[2,128,192]{2,1,0:T(8,128)(2,1)S(1)}) custom-call(bf16[384,1536]{1,0:T(8,128)(2,1)S(1)} %bitcast.23, bf16[1536,1024]{1,0:T(8,128)(2,1)S(1)} %bitcast.27, bf16[1536,1024]{1,0:T(8,128)(2,1)S(1)} %bitcast.28, bf16[1024,1536]{1,0:T(8,128)(2,1)S(1)} %bitcast.29, bf16[1536,1024]{1,0:T(8,128)(2,1)S(1)} %bitcast.26, ...), custom_call_target="tpu_custom_call" | custom-call | flops 7247757312 | bytes 20000000 | tf_op jit(solution)/shard_map/experts/pallas_call | solution.py:226
  57.8 0.0 copy-start.1
  57.8 18.1 %all_to_all.22 = bf16[16,24,1536]{2,1,0:T(8,128)(2,1)S(1)} all-to-all(bf16[16,24,1536]{2,1,0:T(8,128)(2,1)S(1)} %bitcast.24), channel_id=1, replica_groups={{1,3,5,7,65,67,69,71,129,131,133,135,193,195,197,199},{9,11,13,15,73,75..., dimensions={0} | all-to-all | bytes 2359296 | tf_op jit(solution)/shard_map/all_to_all | solution.py:201
  75.9 0.5 gather.1
  76.4 15.9 %all_to_all.23 = bf16[8,24,1536]{2,1,0:T(8,128)(2,1)S(1)} all-to-all(bf16[8,24,1536]{2,1,0:T(8,128)(2,1)S(1)} %bitcast.21), channel_id=1, replica_groups={{1,9,17,25,33,41,49,57},{3,11,19,27,35,43,51,59},{5,13,21,29,37,45,53,6..., dimensions={0} | all-to-all | bytes 1179648 | tf_op jit(solution)/shard_map/all_to_all | solution.py:201
  92.2 0.4 combine.1
  92.6 5.6 %collective-permute-start.3 = (bf16[128,1536]{1,0:T(8,128)(2,1)S(1)}, bf16[128,1536]{1,0:T(8,128)(2,1)S(1)}, u32[]{:S(2)}, u32[]{:S(2)}) collective-permute-start(bf16[128,1536]{1,0:T(8,128)(2,1)S(1)} %combine.1), channel_id=1, source_target_pairs={{0,1},{1,0},{2,3},{3,2},{4,5},{5,4},{6,7},{7,6},{8,9},{9,8},{10,11... | collective-permute-start | bytes 1179656 | tf_op jit(solution)/shard_map/ppermute | solution.py:23
  98.2 1.3 %collective-permute-done.3 = bf16[128,1536]{1,0:T(8,128)(2,1)S(1)} collective-permute-done((bf16[128,1536]{1,0:T(8,128)(2,1)S(1)}, bf16[128,1536]{1,0:T(8,128)(2,1)S(1)}, u32[]{:S(2)}, u32[]{:S(2)}) %collective-permute-start.3) | collective-permute-done | bytes 393248 | tf_op jit(solution)/shard_map/ppermute | solution.py:23
  99.5 0.0 copy-done.1
  99.5 0.9 add_convert_fusion
Async XLA Ops:
  0.0 48.8 %copy-start = (bf16[1,1536,1024]{2,1,0:T(8,128)(2,1)S(1)}, bf16[1,1536,1024]{2,1,0:T(8,128)(2,1)}, u32[]{:S(2)}) copy-start(bf16[1,1536,1024]{2,1,0:T(8,128)(2,1)} %param.12) | copy-start | bytes 9437188
  0.0 24.3 %collective-permute-start = (bf16[1,1536,1024]{2,1,0:T(8,128)(2,1)}, bf16[1,1536,1024]{2,1,0:T(8,128)(2,1)S(1)}, u32[]{:S(2)}, u32[]{:S(2)}) collective-permute-start(bf16[1,1536,1024]{2,1,0:T(8,128)(2,1)} %param.12), channel_id=1, source_target_pairs={{0,1},{1,0},{2,3},{3,2},{4,5},{5,4},{6,7},{7,6},{8,9},{9,8},{10,11... | collective-permute-start | bytes 9437192 | tf_op jit(solution)/shard_map/ppermute | solution.py:23
  3.2 21.1 %collective-permute-start.1 = (bf16[1,1536,1024]{2,1,0:T(8,128)(2,1)}, bf16[1,1536,1024]{2,1,0:T(8,128)(2,1)S(1)}, u32[]{:S(2)}, u32[]{:S(2)}) collective-permute-start(bf16[1,1536,1024]{2,1,0:T(8,128)(2,1)} %param.13), channel_id=1, source_target_pairs={{0,1},{1,0},{2,3},{3,2},{4,5},{5,4},{6,7},{7,6},{8,9},{9,8},{10,11... | collective-permute-start | bytes 9437192 | tf_op jit(solution)/shard_map/ppermute | solution.py:23
  3.2 21.1 %collective-permute-start.2 = (bf16[1,1024,1536]{2,1,0:T(8,128)(2,1)}, bf16[1,1024,1536]{2,1,0:T(8,128)(2,1)S(1)}, u32[]{:S(2)}, u32[]{:S(2)}) collective-permute-start(bf16[1,1024,1536]{2,1,0:T(8,128)(2,1)} %param.14), channel_id=1, source_target_pairs={{0,1},{1,0},{2,3},{3,2},{4,5},{5,4},{6,7},{7,6},{8,9},{9,8},{10,11... | collective-permute-start | bytes 9437192 | tf_op jit(solution)/shard_map/ppermute | solution.py:23
  57.8 41.7 %copy-start.1 = (bf16[128,1536]{1,0:T(8,128)(2,1)S(1)}, bf16[128,1536]{1,0:T(8,128)(2,1)}, u32[]{:S(2)}) copy-start(bf16[128,1536]{1,0:T(8,128)(2,1)} %refs_0_.1) | copy-start | bytes 1179652
  92.6 6.9 %collective-permute-start.3 = (bf16[128,1536]{1,0:T(8,128)(2,1)S(1)}, bf16[128,1536]{1,0:T(8,128)(2,1)S(1)}, u32[]{:S(2)}, u32[]{:S(2)}) collective-permute-start(bf16[128,1536]{1,0:T(8,128)(2,1)S(1)} %combine.1), channel_id=1, source_target_pairs={{0,1},{1,0},{2,3},{3,2},{4,5},{5,4},{6,7},{7,6},{8,9},{9,8},{10,11... | collective-permute-start | bytes 1179656 | tf_op jit(solution)/shard_map/ppermute | solution.py:23

commit v7 on v6

--- a/solution.py
+++ b/solution.py
@@ -115,15 +115,17 @@
         router[...], normed[...], (((1,), (1,)), ((), ())), preferred_element_type=F32
     )
     expert = iota((experts, tokens), 0)
-    score = []
-    for k in range(2):
-        chosen = jnp.sum(jnp.where(expert == ids[k : k + 1, :], logits, 0.0), axis=0, keepdims=True)
-        score.append(1.0 / (1.0 + jnp.exp(-chosen)))
-    total = score[0] + score[1]
+    chosen = [
+        jnp.sum(jnp.where(expert == ids[k : k + 1, :], logits, 0.0), axis=0, keepdims=True)
+        for k in range(2)
+    ]
+    low = jnp.minimum(jnp.minimum(chosen[0], chosen[1]), 0.0)
+    inverse = [jnp.exp(low) + jnp.exp(low - c) for c in chosen]
+    total = inverse[0] + inverse[1]
     slots = slot_numbers(own, ids, pos, keep)
     key = slot_keys(own, tokens)
-    share = jnp.where(key == slots[0:1, :], score[0] / total, 0.0)
-    share = share + jnp.where(key == slots[1:2, :], score[1] / total, 0.0)
+    share = jnp.where(key == slots[0:1, :], inverse[1] / total, 0.0)
+    share = share + jnp.where(key == slots[1:2, :], inverse[0] / total, 0.0)
     share = share.T
     high = share.astype(BF16)
     table[0] = high

time: 101 us -> 101 us (level)
  no operation moved by 1% of the time
where the time goes in v7:
time: 101 us; the launch traced here: 100 us
  blocking collectives  77.2 us (76%)
  Pallas kernels  11.6 us (11%)
  starting transfers between devices  9.3 us (9%)
  waiting for transfers between devices  1.36 us (1%)
    all_to_all x4, blocking collectives, exchange(): lax.all_to_all(cut, ('expert', 'tensor'), 0, 0, axis_index_groups=groups,...  77.2 us
    ppermute x4, starting transfers between devices, swap(): return lax.ppermute(x, 'tensor', SWAP)  9.3 us
    pallas_call x1, Pallas kernels, per_device(): pl.pallas_call(functools.partial(expert_kernel, own), out_shape=(twice, p...  8.95 us
  transfers between devices with their start and end apart: 4, of which 1 were waited for; matrix products, arithmetic and copies ran while one was open for 0% of the time, Pallas kernels for 1%

profile of v7, /device:TPU:1, one launch (start us, length us, event | category | flops | bytes accessed | tf_op | source)
XLA Modules:
  0.0 100.4 jit_solution(17514098191219350938)
XLA Ops:
  0.0 0.0 copy-start
  0.0 3.2 %collective-permute-start = (bf16[1,1536,1024]{2,1,0:T(8,128)(2,1)}, bf16[1,1536,1024]{2,1,0:T(8,128)(2,1)S(1)}, u32[]{:S(2)}, u32[]{:S(2)}) collective-permute-start(bf16[1,1536,1024]{2,1,0:T(8,128)(2,1)} %param.12), channel_id=1, source_target_pairs={{0,1},{1,0},{2,3},{3,2},{4,5},{5,4},{6,7},{7,6},{8,9},{9,8},{10,11... | collective-permute-start | bytes 9437192 | tf_op jit(solution)/shard_map/ppermute | solution.py:23
  3.2 0.0 collective-permute-start.1
  3.2 0.5 collective-permute-start.2
  3.7 1.5 %dispatch.1 = (bf16[128,1536]{1,0:T(8,128)(2,1)S(1)}, bf16[192,1536]{1,0:T(8,128)(2,1)S(1)}) custom-call(bf16[128,1536]{1,0:T(8,128)(2,1)} %refs_0_.1, f32[1536]{0:T(1024)} %refs_1_.1, s32[2,128]{1,0:T(2,128)} %bitcast.30, s32[2,128]{1,0:T(2,128)} %bitcast.32, s32[2,128]{1,0:T(2,128)} %bitcast.34), custom_call_target="tpu_custom_call" | custom-call | tf_op jit(solution)/shard_map/dispatch/pallas_call | solution.py:209
  5.2 19.1 %all_to_all.20 = bf16[8,24,1536]{2,1,0:T(8,128)(2,1)S(1)} all-to-all(bf16[8,24,1536]{2,1,0:T(8,128)(2,1)S(1)} %bitcast.25), channel_id=1, replica_groups={{1,9,17,25,33,41,49,57},{3,11,19,27,35,43,51,59},{5,13,21,29,37,45,53,6..., dimensions={0} | all-to-all | bytes 1179648 | tf_op jit(solution)/shard_map/all_to_all | solution.py:203
  24.3 0.0 collective-permute-done
  24.3 0.0 collective-permute-done.1
  24.3 0.0 collective-permute-done.2
  24.4 0.3 regroup.1
  24.7 24.2 %all_to_all.21 = bf16[16,24,1536]{2,1,0:T(8,128)(2,1)S(1)} all-to-all(bf16[16,24,1536]{2,1,0:T(8,128)(2,1)S(1)} %bitcast.18), channel_id=1, replica_groups={{1,3,5,7,65,67,69,71,129,131,133,135,193,195,197,199},{9,11,13,15,73,75..., dimensions={0} | all-to-all | bytes 2359296 | tf_op jit(solution)/shard_map/all_to_all | solution.py:203
  48.8 0.0 copy-done
  48.8 8.9 %experts.1 = (bf16[384,1536]{1,0:T(8,128)(2,1)S(1)}, bf16[2,128,192]{2,1,0:T(8,128)(2,1)S(1)}) custom-call(bf16[384,1536]{1,0:T(8,128)(2,1)S(1)} %bitcast.23, bf16[1536,1024]{1,0:T(8,128)(2,1)S(1)} %bitcast.27, bf16[1536,1024]{1,0:T(8,128)(2,1)S(1)} %bitcast.28, bf16[1024,1536]{1,0:T(8,128)(2,1)S(1)} %bitcast.29, bf16[1536,1024]{1,0:T(8,128)(2,1)S(1)} %bitcast.26, ...), custom_call_target="tpu_custom_call" | custom-call | flops 7247757312 | bytes 20000000 | tf_op jit(solution)/shard_map/experts/pallas_call | solution.py:228
  57.8 0.0 copy-start.1
  57.8 18.1 %all_to_all.22 = bf16[16,24,1536]{2,1,0:T(8,128)(2,1)S(1)} all-to-all(bf16[16,24,1536]{2,1,0:T(8,128)(2,1)S(1)} %bitcast.24), channel_id=1, replica_groups={{1,3,5,7,65,67,69,71,129,131,133,135,193,195,197,199},{9,11,13,15,73,75..., dimensions={0} | all-to-all | bytes 2359296 | tf_op jit(solution)/shard_map/all_to_all | solution.py:203
  75.9 0.5 gather.1
  76.4 15.9 %all_to_all.23 = bf16[8,24,1536]{2,1,0:T(8,128)(2,1)S(1)} all-to-all(bf16[8,24,1536]{2,1,0:T(8,128)(2,1)S(1)} %bitcast.21), channel_id=1, replica_groups={{1,9,17,25,33,41,49,57},{3,11,19,27,35,43,51,59},{5,13,21,29,37,45,53,6..., dimensions={0} | all-to-all | bytes 1179648 | tf_op jit(solution)/shard_map/all_to_all | solution.py:203
  92.2 0.4 combine.1
  92.6 5.6 %collective-permute-start.3 = (bf16[128,1536]{1,0:T(8,128)(2,1)S(1)}, bf16[128,1536]{1,0:T(8,128)(2,1)S(1)}, u32[]{:S(2)}, u32[]{:S(2)}) collective-permute-start(bf16[128,1536]{1,0:T(8,128)(2,1)S(1)} %combine.1), channel_id=1, source_target_pairs={{0,1},{1,0},{2,3},{3,2},{4,5},{5,4},{6,7},{7,6},{8,9},{9,8},{10,11... | collective-permute-start | bytes 1179656 | tf_op jit(solution)/shard_map/ppermute | solution.py:23
  98.2 1.3 %collective-permute-done.3 = bf16[128,1536]{1,0:T(8,128)(2,1)S(1)} collective-permute-done((bf16[128,1536]{1,0:T(8,128)(2,1)S(1)}, bf16[128,1536]{1,0:T(8,128)(2,1)S(1)}, u32[]{:S(2)}, u32[]{:S(2)}) %collective-permute-start.3) | collective-permute-done | bytes 393248 | tf_op jit(solution)/shard_map/ppermute | solution.py:23
  99.5 0.0 copy-done.1
  99.5 0.9 add_convert_fusion
Async XLA Ops:
  0.0 48.8 %copy-start = (bf16[1,1536,1024]{2,1,0:T(8,128)(2,1)S(1)}, bf16[1,1536,1024]{2,1,0:T(8,128)(2,1)}, u32[]{:S(2)}) copy-start(bf16[1,1536,1024]{2,1,0:T(8,128)(2,1)} %param.12) | copy-start | bytes 9437188
  0.0 24.3 %collective-permute-start = (bf16[1,1536,1024]{2,1,0:T(8,128)(2,1)}, bf16[1,1536,1024]{2,1,0:T(8,128)(2,1)S(1)}, u32[]{:S(2)}, u32[]{:S(2)}) collective-permute-start(bf16[1,1536,1024]{2,1,0:T(8,128)(2,1)} %param.12), channel_id=1, source_target_pairs={{0,1},{1,0},{2,3},{3,2},{4,5},{5,4},{6,7},{7,6},{8,9},{9,8},{10,11... | collective-permute-start | bytes 9437192 | tf_op jit(solution)/shard_map/ppermute | solution.py:23
  3.2 21.1 %collective-permute-start.1 = (bf16[1,1536,1024]{2,1,0:T(8,128)(2,1)}, bf16[1,1536,1024]{2,1,0:T(8,128)(2,1)S(1)}, u32[]{:S(2)}, u32[]{:S(2)}) collective-permute-start(bf16[1,1536,1024]{2,1,0:T(8,128)(2,1)} %param.13), channel_id=1, source_target_pairs={{0,1},{1,0},{2,3},{3,2},{4,5},{5,4},{6,7},{7,6},{8,9},{9,8},{10,11... | collective-permute-start | bytes 9437192 | tf_op jit(solution)/shard_map/ppermute | solution.py:23
  3.2 21.1 %collective-permute-start.2 = (bf16[1,1024,1536]{2,1,0:T(8,128)(2,1)}, bf16[1,1024,1536]{2,1,0:T(8,128)(2,1)S(1)}, u32[]{:S(2)}, u32[]{:S(2)}) collective-permute-start(bf16[1,1024,1536]{2,1,0:T(8,128)(2,1)} %param.14), channel_id=1, source_target_pairs={{0,1},{1,0},{2,3},{3,2},{4,5},{5,4},{6,7},{7,6},{8,9},{9,8},{10,11... | collective-permute-start | bytes 9437192 | tf_op jit(solution)/shard_map/ppermute | solution.py:23
  57.8 41.8 %copy-start.1 = (bf16[128,1536]{1,0:T(8,128)(2,1)S(1)}, bf16[128,1536]{1,0:T(8,128)(2,1)}, u32[]{:S(2)}) copy-start(bf16[128,1536]{1,0:T(8,128)(2,1)} %refs_0_.1) | copy-start | bytes 1179652
  92.6 6.9 %collective-permute-start.3 = (bf16[128,1536]{1,0:T(8,128)(2,1)S(1)}, bf16[128,1536]{1,0:T(8,128)(2,1)S(1)}, u32[]{:S(2)}, u32[]{:S(2)}) collective-permute-start(bf16[128,1536]{1,0:T(8,128)(2,1)S(1)} %combine.1), channel_id=1, source_target_pairs={{0,1},{1,0},{2,3},{3,2},{4,5},{5,4},{6,7},{7,6},{8,9},{9,8},{10,11... | collective-permute-start | bytes 1179656 | tf_op jit(solution)/shard_map/ppermute | solution.py:23

commit v8 on v7

--- a/solution.py
+++ b/solution.py
@@ -101,11 +101,17 @@
 
 def gather_kernel(own, partial, send):
     count = SIDE * own * SIDE
-    shape = (SIDE, own, SIDE, 2 * count)
-    holder = (iota(shape, 2) * 2 * own + iota(shape, 1)) * SIDE + iota(shape, 0)
-    column = iota(shape, 3)
-    pick = ((column == holder) | (column == holder + own * SIDE)).reshape(count, 2 * count)
-    send[...] = dot(jnp.where(pick, 1.0, 0.0).astype(BF16), partial[...]).astype(BF16)
+    size = own * SIDE
+    sums = []
+    for e in range(SIDE):
+        one = partial[2 * e * size : (2 * e + 1) * size, :].astype(F32)
+        two = partial[(2 * e + 1) * size : (2 * e + 2) * size, :].astype(F32)
+        sums.append(one + two)
+    rows = jnp.concatenate(sums, axis=0).astype(BF16)
+    shape = (SIDE, own, SIDE, count)
+    source = (iota(shape, 2) * own + iota(shape, 1)) * SIDE + iota(shape, 0)
+    pick = (source == iota(shape, 3)).reshape(count, count)
+    send[...] = dot(jnp.where(pick, 1.0, 0.0).astype(BF16), rows).astype(BF16)
 
 
 def weigh(own, normed, router, ids, pos, keep, table):

time: 101 us -> 101 us (level)
  no operation moved by 1% of the time
where the time goes in v8:
time: 101 us; the launch traced here: 100 us
  blocking collectives  77.2 us (76%)
  Pallas kernels  11.4 us (11%)
  starting transfers between devices  9.3 us (9%)
  waiting for transfers between devices  1.36 us (1%)
    all_to_all x4, blocking collectives, exchange(): lax.all_to_all(cut, ('expert', 'tensor'), 0, 0, axis_index_groups=groups,...  77.2 us
    ppermute x4, starting transfers between devices, swap(): return lax.ppermute(x, 'tensor', SWAP)  9.3 us
    pallas_call x1, Pallas kernels, per_device(): pl.pallas_call(functools.partial(expert_kernel, own), out_shape=(twice, p...  8.95 us
  transfers between devices with their start and end apart: 4, of which 1 were waited for; matrix products, arithmetic and copies ran while one was open for 0% of the time, Pallas kernels for 1%

profile of v8, /device:TPU:1, one launch (start us, length us, event | category | flops | bytes accessed | tf_op | source)
XLA Modules:
  0.0 100.3 jit_solution(13974533224650646884)
XLA Ops:
  0.0 0.0 copy-start
  0.0 3.2 %collective-permute-start = (bf16[1,1536,1024]{2,1,0:T(8,128)(2,1)}, bf16[1,1536,1024]{2,1,0:T(8,128)(2,1)S(1)}, u32[]{:S(2)}, u32[]{:S(2)}) collective-permute-start(bf16[1,1536,1024]{2,1,0:T(8,128)(2,1)} %param.12), channel_id=1, source_target_pairs={{0,1},{1,0},{2,3},{3,2},{4,5},{5,4},{6,7},{7,6},{8,9},{9,8},{10,11... | collective-permute-start | bytes 9437192 | tf_op jit(solution)/shard_map/ppermute | solution.py:23
  3.2 0.0 collective-permute-start.1
  3.2 0.5 collective-permute-start.2
  3.7 1.5 %dispatch.1 = (bf16[128,1536]{1,0:T(8,128)(2,1)S(1)}, bf16[192,1536]{1,0:T(8,128)(2,1)S(1)}) custom-call(bf16[128,1536]{1,0:T(8,128)(2,1)} %refs_0_.1, f32[1536]{0:T(1024)} %refs_1_.1, s32[2,128]{1,0:T(2,128)} %bitcast.30, s32[2,128]{1,0:T(2,128)} %bitcast.32, s32[2,128]{1,0:T(2,128)} %bitcast.34), custom_call_target="tpu_custom_call" | custom-call | tf_op jit(solution)/shard_map/dispatch/pallas_call | solution.py:215
  5.2 19.1 %all_to_all.20 = bf16[8,24,1536]{2,1,0:T(8,128)(2,1)S(1)} all-to-all(bf16[8,24,1536]{2,1,0:T(8,128)(2,1)S(1)} %bitcast.25), channel_id=1, replica_groups={{1,9,17,25,33,41,49,57},{3,11,19,27,35,43,51,59},{5,13,21,29,37,45,53,6..., dimensions={0} | all-to-all | bytes 1179648 | tf_op jit(solution)/shard_map/all_to_all | solution.py:209
  24.3 0.0 collective-permute-done
  24.3 0.0 collective-permute-done.1
  24.3 0.0 collective-permute-done.2
  24.4 0.3 regroup.1
  24.7 24.2 %all_to_all.21 = bf16[16,24,1536]{2,1,0:T(8,128)(2,1)S(1)} all-to-all(bf16[16,24,1536]{2,1,0:T(8,128)(2,1)S(1)} %bitcast.18), channel_id=1, replica_groups={{1,3,5,7,65,67,69,71,129,131,133,135,193,195,197,199},{9,11,13,15,73,75..., dimensions={0} | all-to-all | bytes 2359296 | tf_op jit(solution)/shard_map/all_to_all | solution.py:209
  48.8 0.0 copy-done
  48.8 8.9 %experts.1 = (bf16[384,1536]{1,0:T(8,128)(2,1)S(1)}, bf16[2,128,192]{2,1,0:T(8,128)(2,1)S(1)}) custom-call(bf16[384,1536]{1,0:T(8,128)(2,1)S(1)} %bitcast.23, bf16[1536,1024]{1,0:T(8,128)(2,1)S(1)} %bitcast.27, bf16[1536,1024]{1,0:T(8,128)(2,1)S(1)} %bitcast.28, bf16[1024,1536]{1,0:T(8,128)(2,1)S(1)} %bitcast.29, bf16[1536,1024]{1,0:T(8,128)(2,1)S(1)} %bitcast.26, ...), custom_call_target="tpu_custom_call" | custom-call | flops 7247757312 | bytes 20000000 | tf_op jit(solution)/shard_map/experts/pallas_call | solution.py:234
  57.8 0.0 copy-start.1
  57.8 18.1 %all_to_all.22 = bf16[16,24,1536]{2,1,0:T(8,128)(2,1)S(1)} all-to-all(bf16[16,24,1536]{2,1,0:T(8,128)(2,1)S(1)} %bitcast.24), channel_id=1, replica_groups={{1,3,5,7,65,67,69,71,129,131,133,135,193,195,197,199},{9,11,13,15,73,75..., dimensions={0} | all-to-all | bytes 2359296 | tf_op jit(solution)/shard_map/all_to_all | solution.py:209
  75.9 0.3 gather.1
  76.2 15.9 %all_to_all.23 = bf16[8,24,1536]{2,1,0:T(8,128)(2,1)S(1)} all-to-all(bf16[8,24,1536]{2,1,0:T(8,128)(2,1)S(1)} %bitcast.21), channel_id=1, replica_groups={{1,9,17,25,33,41,49,57},{3,11,19,27,35,43,51,59},{5,13,21,29,37,45,53,6..., dimensions={0} | all-to-all | bytes 1179648 | tf_op jit(solution)/shard_map/all_to_all | solution.py:209
  92.1 0.4 combine.1
  92.5 5.6 %collective-permute-start.3 = (bf16[128,1536]{1,0:T(8,128)(2,1)S(1)}, bf16[128,1536]{1,0:T(8,128)(2,1)S(1)}, u32[]{:S(2)}, u32[]{:S(2)}) collective-permute-start(bf16[128,1536]{1,0:T(8,128)(2,1)S(1)} %combine.1), channel_id=1, source_target_pairs={{0,1},{1,0},{2,3},{3,2},{4,5},{5,4},{6,7},{7,6},{8,9},{9,8},{10,11... | collective-permute-start | bytes 1179656 | tf_op jit(solution)/shard_map/ppermute | solution.py:23
  98.1 1.3 %collective-permute-done.3 = bf16[128,1536]{1,0:T(8,128)(2,1)S(1)} collective-permute-done((bf16[128,1536]{1,0:T(8,128)(2,1)S(1)}, bf16[128,1536]{1,0:T(8,128)(2,1)S(1)}, u32[]{:S(2)}, u32[]{:S(2)}) %collective-permute-start.3) | collective-permute-done | bytes 393248 | tf_op jit(solution)/shard_map/ppermute | solution.py:23
  99.4 0.0 copy-done.1
  99.4 0.9 add_convert_fusion
Async XLA Ops:
  0.0 48.8 %copy-start = (bf16[1,1536,1024]{2,1,0:T(8,128)(2,1)S(1)}, bf16[1,1536,1024]{2,1,0:T(8,128)(2,1)}, u32[]{:S(2)}) copy-start(bf16[1,1536,1024]{2,1,0:T(8,128)(2,1)} %param.12) | copy-start | bytes 9437188
  0.0 24.3 %collective-permute-start = (bf16[1,1536,1024]{2,1,0:T(8,128)(2,1)}, bf16[1,1536,1024]{2,1,0:T(8,128)(2,1)S(1)}, u32[]{:S(2)}, u32[]{:S(2)}) collective-permute-start(bf16[1,1536,1024]{2,1,0:T(8,128)(2,1)} %param.12), channel_id=1, source_target_pairs={{0,1},{1,0},{2,3},{3,2},{4,5},{5,4},{6,7},{7,6},{8,9},{9,8},{10,11... | collective-permute-start | bytes 9437192 | tf_op jit(solution)/shard_map/ppermute | solution.py:23
  3.2 21.1 %collective-permute-start.1 = (bf16[1,1536,1024]{2,1,0:T(8,128)(2,1)}, bf16[1,1536,1024]{2,1,0:T(8,128)(2,1)S(1)}, u32[]{:S(2)}, u32[]{:S(2)}) collective-permute-start(bf16[1,1536,1024]{2,1,0:T(8,128)(2,1)} %param.13), channel_id=1, source_target_pairs={{0,1},{1,0},{2,3},{3,2},{4,5},{5,4},{6,7},{7,6},{8,9},{9,8},{10,11... | collective-permute-start | bytes 9437192 | tf_op jit(solution)/shard_map/ppermute | solution.py:23
  3.2 21.1 %collective-permute-start.2 = (bf16[1,1024,1536]{2,1,0:T(8,128)(2,1)}, bf16[1,1024,1536]{2,1,0:T(8,128)(2,1)S(1)}, u32[]{:S(2)}, u32[]{:S(2)}) collective-permute-start(bf16[1,1024,1536]{2,1,0:T(8,128)(2,1)} %param.14), channel_id=1, source_target_pairs={{0,1},{1,0},{2,3},{3,2},{4,5},{5,4},{6,7},{7,6},{8,9},{9,8},{10,11... | collective-permute-start | bytes 9437192 | tf_op jit(solution)/shard_map/ppermute | solution.py:23
  57.8 41.6 %copy-start.1 = (bf16[128,1536]{1,0:T(8,128)(2,1)S(1)}, bf16[128,1536]{1,0:T(8,128)(2,1)}, u32[]{:S(2)}) copy-start(bf16[128,1536]{1,0:T(8,128)(2,1)} %refs_0_.1) | copy-start | bytes 1179652
  92.5 6.9 %collective-permute-start.3 = (bf16[128,1536]{1,0:T(8,128)(2,1)S(1)}, bf16[128,1536]{1,0:T(8,128)(2,1)S(1)}, u32[]{:S(2)}, u32[]{:S(2)}) collective-permute-start(bf16[128,1536]{1,0:T(8,128)(2,1)S(1)} %combine.1), channel_id=1, source_target_pairs={{0,1},{1,0},{2,3},{3,2},{4,5},{5,4},{6,7},{7,6},{8,9},{9,8},{10,11... | collective-permute-start | bytes 1179656 | tf_op jit(solution)/shard_map/ppermute | solution.py:23
